TPU v7x, 32 devices: a whole 2x2x4 slice. The times are simulated.
32 devices in a mesh: obs: 2 (over y), bt: 4 (over z), freq: 2 (over x), pol: 2 (over core).
Axes of the slice: x: 2, y: 2, z: 4, core: 2. Of those that a mesh axis runs over, the one named last changes fastest.
Arguments:
- gains: float32 [16, 4, 8, 1984], P(('obs', 'bt', 'pol'), 'freq'), parts along dimension 0, may hold values from -3 to 3
- visibilities: bfloat16 [16, 4, 8, 4096], P('obs', 'freq', None, ('bt', 'pol')), parts along dimension 0, may hold values from -6 to 6
- first_station: int32 [8192], P(('obs', 'bt', 'pol')), parts along dimension 0, may hold values from 0 to 61
- second_station: int32 [8192], P(('obs', 'bt', 'pol')), parts along dimension 0, may hold values from 0 to 61, as said below
- filled_row_count: int32 [16], P(('obs', 'bt', 'pol')), parts along dimension 0, may hold values from 256 to 512
- facet_dir: int32 [16], P('obs'), parts along dimension 0, may hold values from 0 to 7, each once
Outputs:
- corrected: bfloat16 [16, 4, 8, 4096], P('obs', 'freq', None, ('bt', 'pol')), parts along dimension 0
There are 2 independent parts, one for each index of `obs`. A program takes and returns all parts, laid end to end along the dimension named above; each array names one. Nothing has to cross between parts.
Inputs may be any that keep to these rules, and one draw needn't show every extreme that they name: In every row second_station differs from first_station. `facet_dir`: each direction names exactly one facet.
All inputs are finite; a program needn't handle non-finite values.
Results may differ from a plain program's by a relative error of at most 0.001.
Values sent between devices are 32-bit elements; how exact they have to be, the bound alone decides.
No kernel may reach another device: no remote copies, remote signals or barrier semaphores. Data moves between devices by JAX's collectives and lax.ppermute only.
A program may use at most 64 MiB of HBM per device.

v0:
```python
import jax
import jax.numpy as jnp
from jax import lax
from jax.sharding import PartitionSpec as P

ARRAY_STATIONS = 62
GAIN_SLOT_COUNT = 4


def entry(values, row_at, col_at):
    return (values[..., 2 * row_at + col_at, :], values[..., 4 + 2 * row_at + col_at, :])


def apply_jones(left_matrix, data, right_matrix):
    real_parts = []
    imag_parts = []
    for out_row in (0, 1):
        for out_col in (0, 1):
            total_re = jnp.zeros_like(left_matrix[..., 0, :])
            total_im = jnp.zeros_like(left_matrix[..., 0, :])
            for middle in (0, 1):
                for column in (0, 1):
                    left_re, left_im = entry(left_matrix, out_row, middle)
                    data_re, data_im = entry(data, middle, column)
                    right_re, right_im = entry(right_matrix, out_col, column)
                    prod_re = left_re * data_re - left_im * data_im
                    prod_im = left_re * data_im + left_im * data_re
                    total_re = total_re + prod_re * right_re + prod_im * right_im
                    total_im = total_im + prod_im * right_re - prod_re * right_im
            real_parts.append(total_re)
            imag_parts.append(total_im)
    return jnp.stack(real_parts + imag_parts, axis=-2)


def expand_slots(gain_window, antenna, block_rows, slots, stations):
    facets, chans, comps, _ = gain_window.shape
    current = gain_window[..., : slots * stations].reshape(facets, chans, comps, slots, stations)
    following = gain_window[..., stations:].reshape(facets, chans, comps, slots, stations)
    paired = jnp.concatenate([current, following], axis=4)
    per_slot = block_rows // slots
    grouped = antenna.reshape(slots, per_slot)
    fraction = (jnp.arange(per_slot, dtype=jnp.int32).astype(jnp.float32) + 0.5) / per_slot
    station_ids = jnp.arange(stations, dtype=jnp.int32)
    station_mask = (station_ids[None, :, None] == grouped[:, None, :]).astype(jnp.float32)
    table = jnp.concatenate([station_mask * (1.0 - fraction), station_mask * fraction], axis=1)
    spread = jnp.einsum("fckjn,jnp->fckjp", paired, table, precision=lax.Precision.HIGHEST)
    return spread.reshape(facets, chans, comps, block_rows)


def apply_correction(
    gain_window, block_visibilities, first_station_gain, second_station_gain, filled_rows
):
    block_rows = block_visibilities.shape[3]
    left_matrix = expand_slots(
        gain_window, first_station_gain, block_rows, GAIN_SLOT_COUNT, ARRAY_STATIONS
    )
    right_matrix = expand_slots(
        gain_window, second_station_gain, block_rows, GAIN_SLOT_COUNT, ARRAY_STATIONS
    )
    product = apply_jones(left_matrix, block_visibilities.astype(jnp.float32), right_matrix)
    live_mask = jnp.arange(block_rows, dtype=jnp.int32) < filled_rows
    return jnp.where(live_mask, product, 0.0 * product).astype(jnp.bfloat16)


def relay(payload):
    relaid = lax.all_to_all(payload, ("bt", "pol"), split_axis=3, concat_axis=0, tiled=True)
    return relaid


def select_facets(relaid, facet_dir):
    directions = relaid.shape[0]
    onehot = (facet_dir[:, None] == jnp.arange(directions, dtype=jnp.int32)[None, :]).astype(
        jnp.float32
    )
    return jnp.einsum("fd,dckn->fckn", onehot, relaid, precision=lax.Precision.HIGHEST)


def shards(gains, visibilities, first_station, second_station, filled_row_count, facet_dir):
    block_count = lax.axis_size(("bt", "pol"))
    dirs_here, chans_here, comps, _ = gains.shape
    by_slot = gains.reshape(
        dirs_here, chans_here, comps, block_count, GAIN_SLOT_COUNT, ARRAY_STATIONS
    )
    firsts = by_slot[:, :, :, :, 0, :]
    final_one = by_slot[:, :, :, block_count - 1 :, GAIN_SLOT_COUNT - 1, :]
    nexts = jnp.concatenate([firsts[:, :, :, 1:, :], final_one], axis=3)
    own_slots = by_slot.reshape(
        dirs_here, chans_here, comps, block_count, GAIN_SLOT_COUNT * ARRAY_STATIONS
    )
    windows = jnp.concatenate([own_slots, nexts], axis=4)
    windows = windows.reshape(
        dirs_here, chans_here, comps, block_count * (GAIN_SLOT_COUNT + 1) * ARRAY_STATIONS
    )
    gain_window = select_facets(relay(windows), facet_dir)
    return apply_correction(
        gain_window, visibilities, first_station, second_station, filled_row_count[0]
    )


def solution(mesh):
    return jax.shard_map(
        shards,
        mesh=mesh,
        in_specs=(
            P(("obs", "bt", "pol"), "freq", None, None),
            P("obs", "freq", None, ("bt", "pol")),
            P(("obs", "bt", "pol")),
            P(("obs", "bt", "pol")),
            P(("obs", "bt", "pol")),
            P("obs"),
        ),
        out_specs=P("obs", "freq", None, ("bt", "pol")),
        check_vma=False,
    )
```

profile of v0, /device:TPU:0, one launch (start us, length us, event | category | flops | bytes accessed | tf_op | source)
XLA Modules:
  0.0 31.5 jit_solution(10585168810742284929)
XLA Ops:
  0.0 1.3 %reshape.32 = f32[1,2,8,8,4,62]{5,4,3,2,1,0:T(4,128)S(1)} reshape(f32[1,2,8,1984]{3,2,1,0:T(8,128)} %param.6) | data formatting | bytes 253952 | tf_op jit(solution)/shard_map/reshape | solution.py:81
  1.4 1.0 %reshape_reshape.3 = f32[1,2,8,8,248]{4,3,2,1,0:T(8,128)S(1)} reshape(f32[1,2,8,1984]{3,2,1,0:T(8,128)} %param.6) | data formatting | bytes 253952 | tf_op jit(solution)/shard_map/reshape;reshape | solution.py:87
  2.4 0.1 maximum_maximum_fusion
  2.6 2.2 %copy.38 = f32[1,2,8,8,310]{2,1,4,3,0:T(2,128)S(1)} copy(f32[1,2,8,8,310]{4,3,2,1,0:T(8,128)S(1)} %maximum_maximum_fusion) | data formatting | bytes 317440 | tf_op jit(solution)/shard_map/concatenate | solution.py:90
  4.8 4.0 %reshape.41 = f32[8,1,4960]{2,1,0:T(1,128)} reshape(f32[2480,1,2,8]{3,2,1,0:T(2,128)S(1)} %bitcast.55) | data formatting | bytes 317440
  8.8 6.4 %all-to-all-start = ((f32[8,1,4960]{2,1,0:T(1,128)}), f32[8,1,4960]{2,1,0:T(1,128)S(1)}, u32[]{:S(2)}, u32[]{:S(2)}) async-start(f32[8,1,4960]{2,1,0:T(1,128)} %reshape.41), calls=%async_computation | async-start | bytes 319488 | tf_op jit(solution)/shard_map/all_to_all | solution.py:66
  16.0 6.3 %all-to-all-done = f32[8,1,4960]{2,1,0:T(1,128)S(1)} async-done(((f32[8,1,4960]{2,1,0:T(1,128)}), f32[8,1,4960]{2,1,0:T(1,128)S(1)}, u32[]{:S(2)}, u32[]{:S(2)}) %all-to-all-start) | async-done | bytes 158752 | tf_op jit(solution)/shard_map/all_to_all | solution.py:66
  22.3 0.5 %broadcast.50 = f32[]{:T(128)} broadcast(f32[]{:T(128)} %constant.71), dimensions={} | broadcast | bytes 8 | tf_op jit(solution)/shard_map/all_to_all | solution.py:66
  22.8 1.0 %reduce = f32[8,4960]{1,0:T(8,128)S(1)} reduce(f32[8,1,4960]{2,1,0:T(1,128)S(1)} %all-to-all-done, f32[]{:T(128)} %broadcast.50), dimensions={1}, to_apply=%all_to_all.13.reduce_sub_computation | reduce | bytes 317444 | tf_op jit(solution)/shard_map/all_to_all | solution.py:66
  23.8 2.0 %reshape.42 = f32[2480,1,2,8]{3,2,1,0:T(2,128)S(1)} reshape(f32[8,4960]{1,0:T(8,128)S(1)} %reduce) | data formatting | bytes 317440
  25.8 2.1 %copy.65 = f32[1,2,8,8,310]{4,3,2,1,0:T(8,128)S(1)} copy(f32[1,2,8,8,310]{2,1,4,3,0:T(2,128)S(1)} %bitcast.56) | data formatting | bytes 317440 | tf_op jit(solution)/shard_map/all_to_all | solution.py:66
  27.9 0.3 fusion.5
  28.2 0.1 fusion.18
  28.3 0.2 reshape.34
  28.5 0.2 copy.40
  28.6 0.2 reshape.35
  28.8 0.2 copy.41
  29.0 0.4 %convolution_bitcast_fusion = f32[8,2,8,4,128]{4,2,1,0,3:T(8,128)S(1)} fusion(f32[4,62,128]{2,1,0:T(8,128)S(1)} %get-tuple-element.44, f32[4,62,128]{2,1,0:T(8,128)S(1)} %get-tuple-element.43, f32[8,2,8,4,62]{4,2,1,0,3:T(8,128)S(1)} %copy.41, f32[8,2,8,4,62]{4,2,1,0,3:T(8,128)S(1)} %copy.40), kind=kOutput, calls=%fused_computation | convolution fusion | flops 97644544 | bytes 770048 | tf_op jit(solution)/shard_map/fckjn,jnp->fckjp/dot_general | solution.py:46
  29.5 0.2 fusion.17
  29.6 0.4 %convolution_bitcast_fusion.1 = f32[8,2,8,4,128]{4,2,1,0,3:T(8,128)S(1)} fusion(f32[4,62,128]{2,1,0:T(8,128)S(1)} %get-tuple-element.45, f32[4,62,128]{2,1,0:T(8,128)S(1)} %get-tuple-element.46, f32[8,2,8,4,62]{4,2,1,0,3:T(8,128)S(1)} %copy.41, f32[8,2,8,4,62]{4,2,1,0,3:T(8,128)S(1)} %copy.40), kind=kOutput, calls=%fused_computation.1 | convolution fusion | flops 97644544 | bytes 770048 | tf_op jit(solution)/shard_map/fckjn,jnp->fckjp/dot_general | solution.py:46
  30.1 0.2 fusion.16
  30.3 0.1 add_dynamic-update-slice_fusion.3
  30.4 0.1 add_dynamic-update-slice_fusion.1
  30.8 0.7 %copy.61 = bf16[8,2,8,512]{3,2,1,0:T(8,128)(2,1)} copy(bf16[8,2,8,512]{3,0,2,1:T(8,128)(2,1)S(1)} %fusion) | data formatting | bytes 262144 | tf_op jit(solution)/shard_map/convert_element_type | solution.py:62
  (24 shorter events, 0.6 us)
Async XLA Ops:
  2.6 12.6 %copy-start = (bf16[8,2,8,512]{3,2,1,0:T(8,128)(2,1)S(1)}, bf16[8,2,8,512]{3,2,1,0:T(8,128)(2,1)}, u32[]{:S(2)}) copy-start(bf16[8,2,8,512]{3,2,1,0:T(8,128)(2,1)} %param.7) | copy-start | bytes 393220
  2.6 13.3 %copy-start.1 = (s32[512]{0:T(512)S(1)}, s32[512]{0:T(512)}, u32[]{:S(2)}) copy-start(s32[512]{0:T(512)} %param.9) | copy-start | bytes 6148
  2.6 13.3 %copy-start.2 = (s32[512]{0:T(512)S(1)}, s32[512]{0:T(512)}, u32[]{:S(2)}) copy-start(s32[512]{0:T(512)} %param.8) | copy-start | bytes 6148
  8.8 13.5 %all-to-all-start = ((f32[8,1,4960]{2,1,0:T(1,128)}), f32[8,1,4960]{2,1,0:T(1,128)S(1)}, u32[]{:S(2)}, u32[]{:S(2)}) async-start(f32[8,1,4960]{2,1,0:T(1,128)} %reshape.41), calls=%async_computation | async-start | bytes 319488 | tf_op jit(solution)/shard_map/all_to_all | solution.py:66
  23.8 4.1 %copy-start.3 = (s32[8]{0:T(128)S(1)}, s32[8]{0:T(128)}, u32[]{:S(2)}) copy-start(s32[8]{0:T(128)} %param.11) | copy-start | bytes 100
where the time goes:
time: 31.8 us; the launch traced here: 31.5 us
  local copies, waits for them, and re-layouts  15 us (47%)
  starting transfers between devices  6.35 us (20%)
  waiting for transfers between devices  6.29 us (20%)
  other arithmetic  1.77 us (6%)
  matrix products  1.16 us (4%)
  between operations  0.94 us (3%)
    all_to_all x1, starting transfers between devices, relay(): lax.all_to_all(payload, ('bt', 'pol'), split_axis=3, concat_axis=0, tiled...  6.35 us
    all_to_all x1, waiting for transfers between devices, relay(): lax.all_to_all(payload, ('bt', 'pol'), split_axis=3, concat_axis=0, tiled...  6.29 us
    unnamed x10, local copies, waits for them, and re-layouts  5.99 us
    all_to_all x2, local copies, waits for them, and re-layouts, relay(): lax.all_to_all(payload, ('bt', 'pol'), split_axis=3, concat_axis=0, tiled...  2.57 us
    concatenate x1, local copies, waits for them, and re-layouts, shards(): windows = jnp.concatenate([own_slots, nexts], axis=4)  2.18 us
    reshape x1, local copies, waits for them, and re-layouts, shards(): gains.reshape(dirs_here, chans_here, comps, block_count, GAIN_SLOT_COUNT,...  1.31 us
    another operation x1, local copies, waits for them, and re-layouts, shards(): by_slot.reshape(dirs_here, chans_here, comps, block_count, GAIN_SLOT_COUN...  1.03 us
    all_to_all x1, other arithmetic, relay(): lax.all_to_all(payload, ('bt', 'pol'), split_axis=3, concat_axis=0, tiled...  1.02 us
  transfers between devices with their start and end apart: 1, of which 1 were waited for; matrix products, arithmetic and copies ran while one was open for 0% of the time, Pallas kernels for 0%

commit v1 on v0

v1 whole, which is shorter than its diff:
```python
import functools

import jax
import jax.numpy as jnp
from jax import lax
from jax.experimental import pallas as pl
from jax.experimental.pallas import tpu as pltpu
from jax.sharding import PartitionSpec as P

ARRAY_STATIONS = 62
GAIN_SLOT_COUNT = 4
PAD_STATIONS = 64
COMPS = 8
LANES = 128


def pack_kernel(*refs, npol, nbt, chans):
    sources = refs[:npol]
    outs = refs[npol : npol + nbt]
    packed = refs[npol + nbt]
    bt = lax.axis_index("bt")
    pol = lax.axis_index("pol")
    rows = chans * COMPS
    width = sources[0].shape[1]
    slots = width // ARRAY_STATIONS
    lane = lax.broadcasted_iota(jnp.int32, (rows, LANES), 1)
    low = lane < ARRAY_STATIONS
    high = (lane >= PAD_STATIONS) & (lane < PAD_STATIONS + ARRAY_STATIONS)
    pair = 2 * ARRAY_STATIONS
    tail = jnp.zeros((rows, LANES - pair), jnp.float32)
    half = jnp.zeros((rows, LANES - ARRAY_STATIONS), jnp.float32)
    for source_at, source in enumerate(sources):
        values = source[...]
        for at in range(slots // 2):
            near = jnp.concatenate([values[:, at * pair : (at + 1) * pair], tail], axis=1)
            far = pltpu.roll(near, PAD_STATIONS - ARRAY_STATIONS, axis=1)
            packed[source_at, :, at * LANES : (at + 1) * LANES] = jnp.where(
                low, near, jnp.where(high, far, 0.0)
            )
        packed[source_at, :, slots // 2 * LANES :] = jnp.concatenate(
            [values[:, width - ARRAY_STATIONS :], half], axis=1
        )
    own = GAIN_SLOT_COUNT * PAD_STATIONS
    window = own + PAD_STATIONS
    for shift in range(nbt):
        block = lax.rem(bt + shift, nbt) * npol + pol
        start = pl.multiple_of(block * own, LANES)
        for source_at in range(npol):
            wide = packed[source_at, :, pl.ds(start, own + LANES)]
            outs[shift][source_at] = jnp.concatenate(
                [wide[c * COMPS : (c + 1) * COMPS, :window] for c in range(chans)], axis=1
            )


def apply_kernel(*refs, npol, nbt, chans, facets, block_rows):
    facet_dir, filled = refs[:2]
    windows = refs[2 : 2 + nbt]
    vis, first, second, out, facet_at, gathered, wide_vis, wide_out = refs[2 + nbt :]
    bt = lax.axis_index("bt")
    pol = lax.axis_index("pol")
    per_slot = block_rows // GAIN_SLOT_COUNT
    for f in range(facets):
        facet_at[facet_dir[f]] = f
    for slot in range(GAIN_SLOT_COUNT):
        wide_vis[slot] = vis[:, slot * LANES : (slot + 1) * LANES].astype(jnp.float32)
    chunks = gathered.shape[0]
    for shift in range(nbt):
        for source_at in range(npol):
            direction = lax.rem(bt - shift + nbt, nbt) * npol + lax.rem(
                pol - source_at + npol, npol
            )
            row = pl.multiple_of(facet_at[direction] * COMPS, COMPS)
            for chunk in range(chunks):
                gathered[chunk, pl.ds(row, COMPS), :] = windows[shift][
                    source_at, :, chunk * LANES : (chunk + 1) * LANES
                ]
    gains = jnp.concatenate(
        [
            jnp.concatenate(
                [gathered[chunk, pl.ds(k, facets, stride=COMPS), :] for k in range(COMPS)], axis=0
            )
            for chunk in range(chunks)
        ],
        axis=1,
    )
    coarse = gains.astype(jnp.bfloat16)
    fine = (gains - coarse.astype(jnp.float32)).astype(jnp.bfloat16)
    window = (GAIN_SLOT_COUNT + 1) * PAD_STATIONS
    station = lax.broadcasted_iota(jnp.int32, (PAD_STATIONS, per_slot), 0)
    position = lax.broadcasted_iota(jnp.int32, (PAD_STATIONS, per_slot), 1)
    fraction = (position.astype(jnp.float32) + 0.5) / per_slot
    rest = 1.0 - fraction
    place = lax.broadcasted_iota(jnp.int32, (facets, per_slot), 1)
    live_rows = filled[0]

    def table_of(row):
        hit = station == row
        return jnp.concatenate(
            [jnp.where(hit, rest, 0.0), jnp.where(hit, fraction, 0.0)], axis=0
        ).astype(jnp.bfloat16)

    for slot in range(GAIN_SLOT_COUNT):
        table = jnp.concatenate(
            [table_of(first[slot : slot + 1, :]), table_of(second[slot : slot + 1, :])], axis=1
        )
        table = jnp.concatenate([table, table], axis=0)
        parts = []
        for c in range(chans):
            start = c * window + slot * PAD_STATIONS
            stop = start + 2 * PAD_STATIONS
            parts.append(
                jnp.concatenate([coarse[:, start:stop], fine[:, start:stop]], axis=1)
            )
        spread = jnp.dot(
            jnp.concatenate(parts, axis=0), table, preferred_element_type=jnp.float32
        )
        live = place + slot * per_slot < live_rows
        for c in range(chans):

            def side(k, at):
                row = (c * COMPS + k) * facets
                return spread[row : row + facets, at * per_slot : (at + 1) * per_slot]

            def seen(k):
                return wide_vis[slot, pl.ds(c * COMPS + k, facets, stride=chans * COMPS), :]

            left = [(side(k, 0), side(k + 4, 0)) for k in range(4)]
            right = [(side(k, 1), side(k + 4, 1)) for k in range(4)]
            data = [(seen(k), seen(k + 4)) for k in range(4)]
            for r in (0, 1):
                turned = []
                for col in (0, 1):
                    a_re, a_im = left[2 * r]
                    b_re, b_im = left[2 * r + 1]
                    u_re, u_im = data[col]
                    v_re, v_im = data[2 + col]
                    turned.append(
                        (
                            (a_re * u_re - a_im * u_im) + (b_re * v_re - b_im * v_im),
                            (a_re * u_im + a_im * u_re) + (b_re * v_im + b_im * v_re),
                        )
                    )
                (p_re, p_im), (q_re, q_im) = turned
                for oc in (0, 1):
                    x_re, x_im = right[2 * oc]
                    y_re, y_im = right[2 * oc + 1]
                    total_re = (p_re * x_re + p_im * x_im) + (q_re * y_re + q_im * y_im)
                    total_im = (p_im * x_re - p_re * x_im) + (q_im * y_re - q_re * y_im)
                    k = 2 * r + oc
                    rows = chans * COMPS
                    wide_out[slot, pl.ds(c * COMPS + k, facets, stride=rows), :] = jnp.where(
                        live, total_re, 0.0
                    )
                    wide_out[slot, pl.ds(c * COMPS + k + 4, facets, stride=rows), :] = jnp.where(
                        live, total_im, 0.0
                    )
    for slot in range(GAIN_SLOT_COUNT):
        out[:, slot * LANES : (slot + 1) * LANES] = wide_out[slot].astype(jnp.bfloat16)


def vmem():
    return pl.BlockSpec(memory_space=pltpu.VMEM)


def smem():
    return pl.BlockSpec(memory_space=pltpu.SMEM)


def shards(gains, visibilities, first_station, second_station, filled_row_count, facet_dir):
    nbt = lax.axis_size("bt")
    npol = lax.axis_size("pol")
    dirs_here, chans, comps, width = gains.shape
    facets, _, _, block_rows = visibilities.shape
    assert dirs_here == 1 and comps == COMPS
    per_slot = block_rows // GAIN_SLOT_COUNT
    assert per_slot == LANES
    slots = width // ARRAY_STATIONS
    window = chans * (GAIN_SLOT_COUNT + 1) * PAD_STATIONS
    flat = gains.reshape(chans * comps, width)
    sources = [flat] + [
        lax.ppermute(flat, "pol", [(i, (i + s) % npol) for i in range(npol)])
        for s in range(1, npol)
    ]
    outgoing = pl.pallas_call(
        functools.partial(pack_kernel, npol=npol, nbt=nbt, chans=chans),
        out_shape=[jax.ShapeDtypeStruct((npol, comps, window), jnp.float32)] * nbt,
        in_specs=[vmem()] * npol,
        out_specs=[vmem()] * nbt,
        scratch_shapes=[
            pltpu.VMEM((npol, chans * comps, slots * PAD_STATIONS + LANES), jnp.float32)
        ],
        name="pack_windows",
    )(*sources)
    arrived = [outgoing[0]] + [
        lax.ppermute(outgoing[k], "bt", [(i, (i + k) % nbt) for i in range(nbt)])
        for k in range(1, nbt)
    ]
    rows = facets * chans * comps
    corrected = pl.pallas_call(
        functools.partial(
            apply_kernel,
            npol=npol,
            nbt=nbt,
            chans=chans,
            facets=facets,
            block_rows=block_rows,
        ),
        out_shape=jax.ShapeDtypeStruct((rows, block_rows), jnp.bfloat16),
        in_specs=[smem(), smem()] + [vmem()] * (nbt + 3),
        out_specs=vmem(),
        scratch_shapes=[
            pltpu.SMEM((facets,), jnp.int32),
            pltpu.VMEM((window // LANES, facets * comps, LANES), jnp.float32),
            pltpu.VMEM((GAIN_SLOT_COUNT, rows, LANES), jnp.float32),
            pltpu.VMEM((GAIN_SLOT_COUNT, rows, LANES), jnp.float32),
        ],
        name="apply_correction",
    )(
        facet_dir,
        filled_row_count,
        *arrived,
        visibilities.reshape(rows, block_rows),
        first_station.reshape(GAIN_SLOT_COUNT, per_slot),
        second_station.reshape(GAIN_SLOT_COUNT, per_slot),
    )
    return corrected.reshape(visibilities.shape)


def solution(mesh):
    return jax.shard_map(
        shards,
        mesh=mesh,
        in_specs=(
            P(("obs", "bt", "pol"), "freq", None, None),
            P("obs", "freq", None, ("bt", "pol")),
            P(("obs", "bt", "pol")),
            P(("obs", "bt", "pol")),
            P(("obs", "bt", "pol")),
            P("obs"),
        ),
        out_specs=P("obs", "freq", None, ("bt", "pol")),
        check_vma=False,
    )
```

time: 31.8 us -> 17.4 us (0.55)
  local copies, waits for them, and re-layouts: 15 us -> 1.27 us
  Pallas kernels: 0 us -> 4.59 us
  waiting for transfers between devices: 6.29 us -> 3.39 us
  other arithmetic: 1.77 us -> 0 us
  matrix products: 1.16 us -> 0 us
  starting transfers between devices: 6.35 us -> 7.35 us
    ppermute x0 -> x4, starting transfers between devices: none -> 7.35 us  [the longest x3 6.86 us: shards(): lax.ppermute(outgoing[k], 'bt', [(i, (i + k) % nbt) for i in range(nbt)])]
    all_to_all x1 -> x0, starting transfers between devices: 6.35 us -> none  [relay(): lax.all_to_all(payload, ('bt', 'pol'), split_axis=3, concat_axis=0, tiled...]
    all_to_all x1 -> x0, waiting for transfers between devices: 6.29 us -> none  [relay(): lax.all_to_all(payload, ('bt', 'pol'), split_axis=3, concat_axis=0, tiled...]
    unnamed x10 -> x8, local copies, waits for them, and re-layouts: 5.99 us -> 1.27 us
    pallas_call x0 -> x2, Pallas kernels: none -> 4.59 us  [the longest x1 2.44 us: shards(): pl.pallas_call(functools.partial(pack_kernel, npol=npol, nbt=nbt, chans=c...]
    ppermute x0 -> x4, waiting for transfers between devices: none -> 3.39 us  [the longest x3 2.19 us: shards(): lax.ppermute(outgoing[k], 'bt', [(i, (i + k) % nbt) for i in range(nbt)])]
    all_to_all x2 -> x0, local copies, waits for them, and re-layouts: 2.57 us -> none  [relay(): lax.all_to_all(payload, ('bt', 'pol'), split_axis=3, concat_axis=0, tiled...]
    concatenate x1 -> x0, local copies, waits for them, and re-layouts: 2.18 us -> none  [shards(): windows = jnp.concatenate([own_slots, nexts], axis=4)]
  transfers between devices with their start and end apart: 1 -> 4, of which waited for: 1 -> 3; matrix products, arithmetic and copies ran while one was open for 0% -> 0% of each run, Pallas kernels for 0% -> 0%
where the time goes in v1:
time: 17.4 us; the launch traced here: 17.3 us
  starting transfers between devices  7.35 us (42%)
  Pallas kernels  4.59 us (26%)
  waiting for transfers between devices  3.39 us (19%)
  local copies, waits for them, and re-layouts  1.27 us (7%)
  between operations  0.68 us (4%)
    ppermute x3, starting transfers between devices, shards(): lax.ppermute(outgoing[k], 'bt', [(i, (i + k) % nbt) for i in range(nbt)])  6.86 us
    pallas_call x1, Pallas kernels, shards(): pl.pallas_call(functools.partial(pack_kernel, npol=npol, nbt=nbt, chans=c...  2.44 us
    ppermute x3, waiting for transfers between devices, shards(): lax.ppermute(outgoing[k], 'bt', [(i, (i + k) % nbt) for i in range(nbt)])  2.19 us
    pallas_call x1, Pallas kernels, shards(): pl.pallas_call(functools.partial(apply_kernel, npol=npol, nbt=nbt, chans=...  2.15 us
    unnamed x8, local copies, waits for them, and re-layouts  1.27 us
    ppermute x1, waiting for transfers between devices, shards(): lax.ppermute(flat, 'pol', [(i, (i + s) % npol) for i in range(npol)])  1.2 us
    ppermute x1, starting transfers between devices, shards(): lax.ppermute(flat, 'pol', [(i, (i + s) % npol) for i in range(npol)])  0.49 us
  transfers between devices with their start and end apart: 4, of which 3 were waited for; matrix products, arithmetic and copies ran while one was open for 0% of the time, Pallas kernels for 0%

profile of v1, /device:TPU:0, one launch (start us, length us, event | category | flops | bytes accessed | tf_op | source)
XLA Modules:
  0.0 17.3 jit_solution(1457294455410244962)
XLA Ops:
  0.0 0.5 %collective-permute-start = (f32[16,1984]{1,0:T(8,128)}, f32[16,1984]{1,0:T(8,128)S(1)}, u32[]{:S(2)}, u32[]{:S(2)}) collective-permute-start(f32[16,1984]{1,0:T(8,128)} %bitcast.5), channel_id=1, source_target_pairs={{0,1},{1,0},{2,3},{3,2},{4,5},{5,4},{6,7},{7,6},{8,9},{9,8},{10,11... | collective-permute-start | bytes 380936 | tf_op jit(solution)/shard_map/ppermute | solution.py:181
  0.5 1.2 %collective-permute-done.refs_1_ = f32[16,1984]{1,0:T(8,128)S(1)} collective-permute-done((f32[16,1984]{1,0:T(8,128)}, f32[16,1984]{1,0:T(8,128)S(1)}, u32[]{:S(2)}, u32[]{:S(2)}) %collective-permute-start) | collective-permute-done | bytes 127008 | tf_op jit(solution)/shard_map/ppermute | solution.py:181
  1.7 0.0 copy-start
  1.7 0.7 %copy-done = f32[16,1984]{1,0:T(8,128)} copy-done((f32[16,1984]{1,0:T(8,128)}, f32[16,1984]{1,0:T(8,128)S(1)}, u32[]{:S(2)}) %copy-start) | copy-done | bytes 127000
  2.3 2.4 %pack_windows.1 = (f32[2,8,640]{2,1,0:T(8,128)}, f32[2,8,640]{2,1,0:T(8,128)}, f32[2,8,640]{2,1,0:T(8,128)}, f32[2,8,640]{2,1,0:T(8,128)}) custom-call(f32[16,1984]{1,0:T(8,128)} %bitcast.6, f32[16,1984]{1,0:T(8,128)} %copy-done), custom_call_target="tpu_custom_call" | custom-call | tf_op jit(solution)/shard_map/pack_windows/pallas_call | solution.py:184
  4.8 2.9 %collective-permute-start.1 = (f32[2,8,640]{2,1,0:T(8,128)}, f32[2,8,640]{2,1,0:T(8,128)S(1)}, u32[]{:S(2)}, u32[]{:S(2)}) collective-permute-start(f32[2,8,640]{2,1,0:T(8,128)} %get-tuple-element.10), channel_id=1, source_target_pairs={{0,4},{4,8},{8,12},{12,0},{1,5},{5,9},{9,13},{13,1},{2,6},{6,10},{... | collective-permute-start | bytes 122888 | tf_op jit(solution)/shard_map/ppermute | solution.py:195
  7.7 2.6 %collective-permute-start.2 = (f32[2,8,640]{2,1,0:T(8,128)}, f32[2,8,640]{2,1,0:T(8,128)S(1)}, u32[]{:S(2)}, u32[]{:S(2)}) collective-permute-start(f32[2,8,640]{2,1,0:T(8,128)} %get-tuple-element.11), channel_id=1, source_target_pairs={{0,8},{4,12},{8,0},{12,4},{1,9},{5,13},{9,1},{13,5},{2,10},{6,14},... | collective-permute-start | bytes 122888 | tf_op jit(solution)/shard_map/ppermute | solution.py:195
  10.3 1.3 %collective-permute-start.3 = (f32[2,8,640]{2,1,0:T(8,128)}, f32[2,8,640]{2,1,0:T(8,128)S(1)}, u32[]{:S(2)}, u32[]{:S(2)}) collective-permute-start(f32[2,8,640]{2,1,0:T(8,128)} %get-tuple-element.12), channel_id=1, source_target_pairs={{0,12},{4,0},{8,4},{12,8},{1,13},{5,1},{9,5},{13,9},{2,14},{6,2},{... | collective-permute-start | bytes 122888 | tf_op jit(solution)/shard_map/ppermute | solution.py:195
  12.3 0.0 collective-permute-done.1.refs_3_
  12.3 0.0 copy-start.1
  12.3 1.7 %collective-permute-done.2.refs_4_ = f32[2,8,640]{2,1,0:T(8,128)S(1)} collective-permute-done((f32[2,8,640]{2,1,0:T(8,128)}, f32[2,8,640]{2,1,0:T(8,128)S(1)}, u32[]{:S(2)}, u32[]{:S(2)}) %collective-permute-start.2) | collective-permute-done | bytes 40992 | tf_op jit(solution)/shard_map/ppermute | solution.py:195
  14.1 0.0 copy-start.2
  14.1 0.5 %collective-permute-done.3.refs_5_ = f32[2,8,640]{2,1,0:T(8,128)S(1)} collective-permute-done((f32[2,8,640]{2,1,0:T(8,128)}, f32[2,8,640]{2,1,0:T(8,128)S(1)}, u32[]{:S(2)}, u32[]{:S(2)}) %collective-permute-start.3) | collective-permute-done | bytes 40992 | tf_op jit(solution)/shard_map/ppermute | solution.py:195
  14.5 0.0 copy-start.3
  14.5 0.0 copy-done.1
  14.5 0.1 copy-done.2
  14.7 0.5 %copy-done.3 = f32[2,8,640]{2,1,0:T(8,128)} copy-done((f32[2,8,640]{2,1,0:T(8,128)}, f32[2,8,640]{2,1,0:T(8,128)S(1)}, u32[]{:S(2)}) %copy-start.3) | copy-done | bytes 40984
  15.1 2.1 %apply_correction.1 = bf16[128,512]{1,0:T(8,128)(2,1)} custom-call(s32[8]{0:T(128)} %refs_0_.1, s32[1]{0:T(128)S(6)} %copy.7.refs_1_, f32[2,8,640]{2,1,0:T(8,128)} %get-tuple-element.9.refs_2_, f32[2,8,640]{2,1,0:T(8,128)} %copy-done.1, f32[2,8,640]{2,1,0:T(8,128)} %copy-done.2, f32[2,8,640]{2,1,0:T(8,128)} %copy-done.3, bf16[128,512]{1,0:T(8,128)(2,1)} %bitcast.7, ...), custom_call_target="tpu_custom_call" | custom-call | tf_op jit(solution)/shard_map/apply_correction/pallas_call | solution.py:199
Async XLA Ops:
  0.0 1.7 %collective-permute-start = (f32[16,1984]{1,0:T(8,128)}, f32[16,1984]{1,0:T(8,128)S(1)}, u32[]{:S(2)}, u32[]{:S(2)}) collective-permute-start(f32[16,1984]{1,0:T(8,128)} %bitcast.5), channel_id=1, source_target_pairs={{0,1},{1,0},{2,3},{3,2},{4,5},{5,4},{6,7},{7,6},{8,9},{9,8},{10,11... | collective-permute-start | bytes 380936 | tf_op jit(solution)/shard_map/ppermute | solution.py:181
  1.7 0.7 %copy-start = (f32[16,1984]{1,0:T(8,128)}, f32[16,1984]{1,0:T(8,128)S(1)}, u32[]{:S(2)}) copy-start(f32[16,1984]{1,0:T(8,128)S(1)} %collective-permute-done.refs_1_) | copy-start | bytes 380932
  4.8 7.5 %collective-permute-start.1 = (f32[2,8,640]{2,1,0:T(8,128)}, f32[2,8,640]{2,1,0:T(8,128)S(1)}, u32[]{:S(2)}, u32[]{:S(2)}) collective-permute-start(f32[2,8,640]{2,1,0:T(8,128)} %get-tuple-element.10), channel_id=1, source_target_pairs={{0,4},{4,8},{8,12},{12,0},{1,5},{5,9},{9,13},{13,1},{2,6},{6,10},{... | collective-permute-start | bytes 122888 | tf_op jit(solution)/shard_map/ppermute | solution.py:195
  7.7 6.3 %collective-permute-start.2 = (f32[2,8,640]{2,1,0:T(8,128)}, f32[2,8,640]{2,1,0:T(8,128)S(1)}, u32[]{:S(2)}, u32[]{:S(2)}) collective-permute-start(f32[2,8,640]{2,1,0:T(8,128)} %get-tuple-element.11), channel_id=1, source_target_pairs={{0,8},{4,12},{8,0},{12,4},{1,9},{5,13},{9,1},{13,5},{2,10},{6,14},... | collective-permute-start | bytes 122888 | tf_op jit(solution)/shard_map/ppermute | solution.py:195
  10.3 4.2 %collective-permute-start.3 = (f32[2,8,640]{2,1,0:T(8,128)}, f32[2,8,640]{2,1,0:T(8,128)S(1)}, u32[]{:S(2)}, u32[]{:S(2)}) collective-permute-start(f32[2,8,640]{2,1,0:T(8,128)} %get-tuple-element.12), channel_id=1, source_target_pairs={{0,12},{4,0},{8,4},{12,8},{1,13},{5,1},{9,5},{13,9},{2,14},{6,2},{... | collective-permute-start | bytes 122888 | tf_op jit(solution)/shard_map/ppermute | solution.py:195
  12.3 2.2 %copy-start.1 = (f32[2,8,640]{2,1,0:T(8,128)}, f32[2,8,640]{2,1,0:T(8,128)S(1)}, u32[]{:S(2)}) copy-start(f32[2,8,640]{2,1,0:T(8,128)S(1)} %collective-permute-done.1.refs_3_) | copy-start | bytes 122884
  14.1 0.6 %copy-start.2 = (f32[2,8,640]{2,1,0:T(8,128)}, f32[2,8,640]{2,1,0:T(8,128)S(1)}, u32[]{:S(2)}) copy-start(f32[2,8,640]{2,1,0:T(8,128)S(1)} %collective-permute-done.2.refs_4_) | copy-start | bytes 122884
  14.5 0.6 %copy-start.3 = (f32[2,8,640]{2,1,0:T(8,128)}, f32[2,8,640]{2,1,0:T(8,128)S(1)}, u32[]{:S(2)}) copy-start(f32[2,8,640]{2,1,0:T(8,128)S(1)} %collective-permute-done.3.refs_5_) | copy-start | bytes 122884

commit v2 on v1

--- a/solution.py
+++ b/solution.py
@@ -6,6 +6,7 @@
 from jax.experimental import pallas as pl
 from jax.experimental.pallas import tpu as pltpu
 from jax.sharding import PartitionSpec as P
+
 
 ARRAY_STATIONS = 62
 GAIN_SLOT_COUNT = 4
@@ -54,8 +55,10 @@
 
 def apply_kernel(*refs, npol, nbt, chans, facets, block_rows):
     facet_dir, filled = refs[:2]
-    windows = refs[2 : 2 + nbt]
-    vis, first, second, out, facet_at, gathered, wide_vis, wide_out = refs[2 + nbt :]
+    kept = refs[2]
+    downs = refs[3 : 2 + nbt]
+    ups = refs[2 + nbt : 1 + 2 * nbt]
+    vis, first, second, out, facet_at, gathered, wide_vis, wide_out = refs[1 + 2 * nbt :]
     bt = lax.axis_index("bt")
     pol = lax.axis_index("pol")
     per_slot = block_rows // GAIN_SLOT_COUNT
@@ -71,9 +74,16 @@
             )
             row = pl.multiple_of(facet_at[direction] * COMPS, COMPS)
             for chunk in range(chunks):
-                gathered[chunk, pl.ds(row, COMPS), :] = windows[shift][
-                    source_at, :, chunk * LANES : (chunk + 1) * LANES
-                ]
+                lanes = slice(chunk * LANES, (chunk + 1) * LANES)
+                if shift == 0:
+                    piece = kept[source_at, :, lanes]
+                else:
+                    piece = jnp.where(
+                        bt >= shift,
+                        ups[shift - 1][source_at, :, lanes],
+                        downs[shift - 1][source_at, :, lanes],
+                    )
+                gathered[chunk, pl.ds(row, COMPS), :] = piece
     gains = jnp.concatenate(
         [
             jnp.concatenate(
@@ -160,6 +170,10 @@
 
 def vmem():
     return pl.BlockSpec(memory_space=pltpu.VMEM)
+
+
+def in_vmem(array):
+    return pltpu.with_memory_space_constraint(array, pltpu.VMEM)
 
 
 def smem():
@@ -183,18 +197,21 @@
     ]
     outgoing = pl.pallas_call(
         functools.partial(pack_kernel, npol=npol, nbt=nbt, chans=chans),
-        out_shape=[jax.ShapeDtypeStruct((npol, comps, window), jnp.float32)] * nbt,
+        out_shape=[pltpu.VMEM((npol, comps, window), jnp.float32)] * nbt,
         in_specs=[vmem()] * npol,
         out_specs=[vmem()] * nbt,
         scratch_shapes=[
             pltpu.VMEM((npol, chans * comps, slots * PAD_STATIONS + LANES), jnp.float32)
         ],
         name="pack_windows",
-    )(*sources)
-    arrived = [outgoing[0]] + [
-        lax.ppermute(outgoing[k], "bt", [(i, (i + k) % nbt) for i in range(nbt)])
-        for k in range(1, nbt)
-    ]
+    )(*[in_vmem(s) for s in sources])
+    downs, ups = [], []
+    for k in range(1, nbt):
+        pairs = [(i, i + k - nbt) for i in range(nbt - k, nbt)]
+        downs.append(lax.ppermute(outgoing[k], "bt", pairs))
+        pairs = [(i, i + k) for i in range(nbt - k)]
+        ups.append(lax.ppermute(outgoing[k], "bt", pairs))
+    arrived = [in_vmem(a) for a in [outgoing[0], *downs, *ups]]
     rows = facets * chans * comps
     corrected = pl.pallas_call(
         functools.partial(
@@ -206,7 +223,7 @@
             block_rows=block_rows,
         ),
         out_shape=jax.ShapeDtypeStruct((rows, block_rows), jnp.bfloat16),
-        in_specs=[smem(), smem()] + [vmem()] * (nbt + 3),
+        in_specs=[smem(), smem()] + [vmem()] * (2 * nbt + 2),
         out_specs=vmem(),
         scratch_shapes=[
             pltpu.SMEM((facets,), jnp.int32),
@@ -219,9 +236,9 @@
         facet_dir,
         filled_row_count,
         *arrived,
-        visibilities.reshape(rows, block_rows),
-        first_station.reshape(GAIN_SLOT_COUNT, per_slot),
-        second_station.reshape(GAIN_SLOT_COUNT, per_slot),
+        in_vmem(visibilities.reshape(rows, block_rows)),
+        in_vmem(first_station.reshape(GAIN_SLOT_COUNT, per_slot)),
+        in_vmem(second_station.reshape(GAIN_SLOT_COUNT, per_slot)),
     )
     return corrected.reshape(visibilities.shape)
 

time: 17.4 us -> 31.4 us (1.80)
  starting transfers between devices: 7.35 us -> 21 us
  Pallas kernels: 4.59 us -> 2.62 us
  waiting for transfers between devices: 3.39 us -> 5.12 us
  local copies, waits for them, and re-layouts: 1.27 us -> 1.6 us
    ppermute x3 -> x6, starting transfers between devices: 6.86 us -> 20.5 us  [the longest x3 16.6 us: shards(): ups.append(lax.ppermute(outgoing[k], 'bt', pairs))]
    ppermute x3 -> x6, waiting for transfers between devices: 2.19 us -> 3.92 us  [the longest x3 3.91 us: shards(): downs.append(lax.ppermute(outgoing[k], 'bt', pairs))]
    pallas_call x1, Pallas kernels: 2.44 us -> 0.84 us  [shards(): pl.pallas_call(functools.partial(pack_kernel, npol=npol, nbt=nbt, chans=c...]
    pallas_call x1, Pallas kernels: 2.15 us -> 1.78 us  [shards(): pl.pallas_call(functools.partial(apply_kernel, npol=npol, nbt=nbt, chans=...]
    unnamed x8, local copies, waits for them, and re-layouts: 1.27 us -> 1.6 us
  transfers between devices with their start and end apart: 4 -> 7, of which waited for: 3 -> 2; matrix products, arithmetic and copies ran while one was open for 0% -> 0% of each run, Pallas kernels for 0% -> 0%
where the time goes in v2:
time: 31.4 us; the launch traced here: 31.1 us
  starting transfers between devices  21 us (67%)
  waiting for transfers between devices  5.12 us (16%)
  Pallas kernels  2.62 us (8%)
  local copies, waits for them, and re-layouts  1.6 us (5%)
  between operations  0.75 us (2%)
    ppermute x3, starting transfers between devices, shards(): ups.append(lax.ppermute(outgoing[k], 'bt', pairs))  16.6 us
    ppermute x3, waiting for transfers between devices, shards(): downs.append(lax.ppermute(outgoing[k], 'bt', pairs))  3.91 us
    ppermute x3, starting transfers between devices, shards(): downs.append(lax.ppermute(outgoing[k], 'bt', pairs))  3.88 us
    pallas_call x1, Pallas kernels, shards(): pl.pallas_call(functools.partial(apply_kernel, npol=npol, nbt=nbt, chans=...  1.78 us
    unnamed x8, local copies, waits for them, and re-layouts  1.6 us
    ppermute x1, waiting for transfers between devices, shards(): lax.ppermute(flat, 'pol', [(i, (i + s) % npol) for i in range(npol)])  1.2 us
    pallas_call x1, Pallas kernels, shards(): pl.pallas_call(functools.partial(pack_kernel, npol=npol, nbt=nbt, chans=c...  0.84 us
  transfers between devices with their start and end apart: 7, of which 2 were waited for; matrix products, arithmetic and copies ran while one was open for 0% of the time, Pallas kernels for 0%

profile of v2, /device:TPU:0, one launch (start us, length us, event | category | flops | bytes accessed | tf_op | source)
XLA Modules:
  0.0 31.1 jit_solution(5943614202323215889)
XLA Ops:
  0.0 0.5 %collective-permute-start = (f32[16,1984]{1,0:T(8,128)}, f32[16,1984]{1,0:T(8,128)S(1)}, u32[]{:S(2)}, u32[]{:S(2)}) collective-permute-start(f32[16,1984]{1,0:T(8,128)} %bitcast.5), channel_id=1, source_target_pairs={{0,1},{1,0},{2,3},{3,2},{4,5},{5,4},{6,7},{7,6},{8,9},{9,8},{10,11... | collective-permute-start | bytes 380936 | tf_op jit(solution)/shard_map/ppermute | solution.py:195
  0.5 1.2 %collective-permute-done.refs_1_ = f32[16,1984]{1,0:T(8,128)S(1)} collective-permute-done((f32[16,1984]{1,0:T(8,128)}, f32[16,1984]{1,0:T(8,128)S(1)}, u32[]{:S(2)}, u32[]{:S(2)}) %collective-permute-start) | collective-permute-done | bytes 127008 | tf_op jit(solution)/shard_map/ppermute | solution.py:195
  1.7 0.0 copy-start
  1.7 0.9 %copy-done = f32[1,2,8,1984]{3,2,1,0:T(8,128)S(1)} copy-done((f32[1,2,8,1984]{3,2,1,0:T(8,128)S(1)}, f32[1,2,8,1984]{3,2,1,0:T(8,128)}, u32[]{:S(2)}) %copy-start) | copy-done | bytes 127000
  2.6 0.0 copy-start.1
  2.6 0.8 %pack_windows.1 = (f32[2,8,640]{2,1,0:T(8,128)S(1)}, f32[2,8,640]{2,1,0:T(8,128)S(1)}, f32[2,8,640]{2,1,0:T(8,128)S(1)}, f32[2,8,640]{2,1,0:T(8,128)S(1)}) custom-call(f32[16,1984]{1,0:T(8,128)S(1)} %bitcast.6, f32[16,1984]{1,0:T(8,128)S(1)} %collective-permute-done.refs_1_), custom_call_target="tpu_custom_call" | custom-call | tf_op jit(solution)/shard_map/pack_windows/pallas_call | solution.py:198
  3.4 4.8 %collective-permute-start.4 = (f32[2,8,640]{2,1,0:T(8,128)S(1)}, f32[2,8,640]{2,1,0:T(8,128)S(1)}, u32[]{:S(2)}, u32[]{:S(2)}) collective-permute-start(f32[2,8,640]{2,1,0:T(8,128)S(1)} %get-tuple-element.10), channel_id=1, source_target_pairs={{0,4},{4,8},{8,12},{1,5},{5,9},{9,13},{2,6},{6,10},{10,14},{3,7},{... | collective-permute-start | bytes 122888 | tf_op jit(solution)/shard_map/ppermute | solution.py:213
  8.3 1.3 %collective-permute-start.1 = (f32[2,8,640]{2,1,0:T(8,128)S(1)}, f32[2,8,640]{2,1,0:T(8,128)S(1)}, u32[]{:S(2)}, u32[]{:S(2)}) collective-permute-start(f32[2,8,640]{2,1,0:T(8,128)S(1)} %get-tuple-element.10), channel_id=1, source_target_pairs={{12,0},{13,1},{14,2},{15,3},{28,16},{29,17},{30,18},{31,19}} | collective-permute-start | bytes 122888 | tf_op jit(solution)/shard_map/ppermute | solution.py:211
  9.6 3.9 %collective-permute-start.5 = (f32[2,8,640]{2,1,0:T(8,128)S(1)}, f32[2,8,640]{2,1,0:T(8,128)S(1)}, u32[]{:S(2)}, u32[]{:S(2)}) collective-permute-start(f32[2,8,640]{2,1,0:T(8,128)S(1)} %get-tuple-element.11), channel_id=1, source_target_pairs={{0,8},{4,12},{1,9},{5,13},{2,10},{6,14},{3,11},{7,15},{16,24},{20,... | collective-permute-start | bytes 122888 | tf_op jit(solution)/shard_map/ppermute | solution.py:213
  13.5 1.3 %collective-permute-start.2 = (f32[2,8,640]{2,1,0:T(8,128)S(1)}, f32[2,8,640]{2,1,0:T(8,128)S(1)}, u32[]{:S(2)}, u32[]{:S(2)}) collective-permute-start(f32[2,8,640]{2,1,0:T(8,128)S(1)} %get-tuple-element.11), channel_id=1, source_target_pairs={{8,0},{12,4},{9,1},{13,5},{10,2},{14,6},{11,3},{15,7},{24,16},{28,... | collective-permute-start | bytes 122888 | tf_op jit(solution)/shard_map/ppermute | solution.py:211
  14.8 7.9 %collective-permute-start.6 = (f32[2,8,640]{2,1,0:T(8,128)S(1)}, f32[2,8,640]{2,1,0:T(8,128)S(1)}, u32[]{:S(2)}, u32[]{:S(2)}) collective-permute-start(f32[2,8,640]{2,1,0:T(8,128)S(1)} %get-tuple-element.12), channel_id=1, source_target_pairs={{0,12},{1,13},{2,14},{3,15},{16,28},{17,29},{18,30},{19,31}} | collective-permute-start | bytes 122888 | tf_op jit(solution)/shard_map/ppermute | solution.py:213
  22.7 0.0 collective-permute-done.4.refs_6_
  22.7 1.3 %collective-permute-start.3 = (f32[2,8,640]{2,1,0:T(8,128)S(1)}, f32[2,8,640]{2,1,0:T(8,128)S(1)}, u32[]{:S(2)}, u32[]{:S(2)}) collective-permute-start(f32[2,8,640]{2,1,0:T(8,128)S(1)} %get-tuple-element.12), channel_id=1, source_target_pairs={{4,0},{8,4},{12,8},{5,1},{9,5},{13,9},{6,2},{10,6},{14,10},{7,3},{... | collective-permute-start | bytes 122888 | tf_op jit(solution)/shard_map/ppermute | solution.py:211
  24.6 0.0 collective-permute-done.1.refs_3_
  24.7 0.0 collective-permute-done.5.refs_7_
  24.7 0.0 collective-permute-done.2.refs_4_
  24.7 0.0 collective-permute-done.6.refs_8_
  24.7 3.9 %collective-permute-done.3.refs_5_ = f32[2,8,640]{2,1,0:T(8,128)S(1)} collective-permute-done((f32[2,8,640]{2,1,0:T(8,128)S(1)}, f32[2,8,640]{2,1,0:T(8,128)S(1)}, u32[]{:S(2)}, u32[]{:S(2)}) %collective-permute-start.3) | collective-permute-done | bytes 40992 | tf_op jit(solution)/shard_map/ppermute | solution.py:211
  28.6 0.0 copy-start.3
  28.6 0.0 copy-start.2
  28.6 0.0 copy-done.1
  28.6 0.7 %copy-done.3 = s32[512]{0:T(512)S(1)} copy-done((s32[512]{0:T(512)S(1)}, s32[512]{0:T(512)}, u32[]{:S(2)}) %copy-start.3) | copy-done | bytes 2072
  29.3 0.0 copy-done.2
  29.3 1.8 %apply_correction.1 = bf16[128,512]{1,0:T(8,128)(2,1)} custom-call(s32[8]{0:T(128)} %refs_0_.1, s32[1]{0:T(128)S(6)} %copy.7.refs_1_, f32[2,8,640]{2,1,0:T(8,128)S(1)} %get-tuple-element.9.refs_2_, f32[2,8,640]{2,1,0:T(8,128)S(1)} %collective-permute-done.1.refs_3_, f32[2,8,640]{2,1,0:T(8,128)S(1)} %collective-permute-done.2.refs_4_, ...), custom_call_target="tpu_custom_call" | custom-call | tf_op jit(solution)/shard_map/apply_correction/pallas_call | solution.py:216
Async XLA Ops:
  0.0 1.7 %collective-permute-start = (f32[16,1984]{1,0:T(8,128)}, f32[16,1984]{1,0:T(8,128)S(1)}, u32[]{:S(2)}, u32[]{:S(2)}) collective-permute-start(f32[16,1984]{1,0:T(8,128)} %bitcast.5), channel_id=1, source_target_pairs={{0,1},{1,0},{2,3},{3,2},{4,5},{5,4},{6,7},{7,6},{8,9},{9,8},{10,11... | collective-permute-start | bytes 380936 | tf_op jit(solution)/shard_map/ppermute | solution.py:195
  1.7 0.9 %copy-start = (f32[1,2,8,1984]{3,2,1,0:T(8,128)S(1)}, f32[1,2,8,1984]{3,2,1,0:T(8,128)}, u32[]{:S(2)}) copy-start(f32[1,2,8,1984]{3,2,1,0:T(8,128)} %param.6) | copy-start | bytes 380932
  2.6 26.0 %copy-start.1 = (bf16[8,2,8,512]{3,2,1,0:T(8,128)(2,1)S(1)}, bf16[8,2,8,512]{3,2,1,0:T(8,128)(2,1)}, u32[]{:S(2)}) copy-start(bf16[8,2,8,512]{3,2,1,0:T(8,128)(2,1)} %param.7) | copy-start | bytes 393220
  3.4 19.2 %collective-permute-start.4 = (f32[2,8,640]{2,1,0:T(8,128)S(1)}, f32[2,8,640]{2,1,0:T(8,128)S(1)}, u32[]{:S(2)}, u32[]{:S(2)}) collective-permute-start(f32[2,8,640]{2,1,0:T(8,128)S(1)} %get-tuple-element.10), channel_id=1, source_target_pairs={{0,4},{4,8},{8,12},{1,5},{5,9},{9,13},{2,6},{6,10},{10,14},{3,7},{... | collective-permute-start | bytes 122888 | tf_op jit(solution)/shard_map/ppermute | solution.py:213
  8.3 16.4 %collective-permute-start.1 = (f32[2,8,640]{2,1,0:T(8,128)S(1)}, f32[2,8,640]{2,1,0:T(8,128)S(1)}, u32[]{:S(2)}, u32[]{:S(2)}) collective-permute-start(f32[2,8,640]{2,1,0:T(8,128)S(1)} %get-tuple-element.10), channel_id=1, source_target_pairs={{12,0},{13,1},{14,2},{15,3},{28,16},{29,17},{30,18},{31,19}} | collective-permute-start | bytes 122888 | tf_op jit(solution)/shard_map/ppermute | solution.py:211
  9.6 15.1 %collective-permute-start.5 = (f32[2,8,640]{2,1,0:T(8,128)S(1)}, f32[2,8,640]{2,1,0:T(8,128)S(1)}, u32[]{:S(2)}, u32[]{:S(2)}) collective-permute-start(f32[2,8,640]{2,1,0:T(8,128)S(1)} %get-tuple-element.11), channel_id=1, source_target_pairs={{0,8},{4,12},{1,9},{5,13},{2,10},{6,14},{3,11},{7,15},{16,24},{20,... | collective-permute-start | bytes 122888 | tf_op jit(solution)/shard_map/ppermute | solution.py:213
  13.5 11.2 %collective-permute-start.2 = (f32[2,8,640]{2,1,0:T(8,128)S(1)}, f32[2,8,640]{2,1,0:T(8,128)S(1)}, u32[]{:S(2)}, u32[]{:S(2)}) collective-permute-start(f32[2,8,640]{2,1,0:T(8,128)S(1)} %get-tuple-element.11), channel_id=1, source_target_pairs={{8,0},{12,4},{9,1},{13,5},{10,2},{14,6},{11,3},{15,7},{24,16},{28,... | collective-permute-start | bytes 122888 | tf_op jit(solution)/shard_map/ppermute | solution.py:211
  14.8 9.9 %collective-permute-start.6 = (f32[2,8,640]{2,1,0:T(8,128)S(1)}, f32[2,8,640]{2,1,0:T(8,128)S(1)}, u32[]{:S(2)}, u32[]{:S(2)}) collective-permute-start(f32[2,8,640]{2,1,0:T(8,128)S(1)} %get-tuple-element.12), channel_id=1, source_target_pairs={{0,12},{1,13},{2,14},{3,15},{16,28},{17,29},{18,30},{19,31}} | collective-permute-start | bytes 122888 | tf_op jit(solution)/shard_map/ppermute | solution.py:213
  22.7 5.9 %collective-permute-start.3 = (f32[2,8,640]{2,1,0:T(8,128)S(1)}, f32[2,8,640]{2,1,0:T(8,128)S(1)}, u32[]{:S(2)}, u32[]{:S(2)}) collective-permute-start(f32[2,8,640]{2,1,0:T(8,128)S(1)} %get-tuple-element.12), channel_id=1, source_target_pairs={{4,0},{8,4},{12,8},{5,1},{9,5},{13,9},{6,2},{10,6},{14,10},{7,3},{... | collective-permute-start | bytes 122888 | tf_op jit(solution)/shard_map/ppermute | solution.py:211
  28.6 0.7 %copy-start.3 = (s32[512]{0:T(512)S(1)}, s32[512]{0:T(512)}, u32[]{:S(2)}) copy-start(s32[512]{0:T(512)} %param.9) | copy-start | bytes 6148
  28.6 0.7 %copy-start.2 = (s32[512]{0:T(512)S(1)}, s32[512]{0:T(512)}, u32[]{:S(2)}) copy-start(s32[512]{0:T(512)} %param.8) | copy-start | bytes 6148

commit v3 on v1

--- a/solution.py
+++ b/solution.py
@@ -7,6 +7,7 @@
 from jax.experimental.pallas import tpu as pltpu
 from jax.sharding import PartitionSpec as P
 
+
 ARRAY_STATIONS = 62
 GAIN_SLOT_COUNT = 4
 PAD_STATIONS = 64
@@ -14,14 +15,8 @@
 LANES = 128
 
 
-def pack_kernel(*refs, npol, nbt, chans):
-    sources = refs[:npol]
-    outs = refs[npol : npol + nbt]
-    packed = refs[npol + nbt]
-    bt = lax.axis_index("bt")
-    pol = lax.axis_index("pol")
-    rows = chans * COMPS
-    width = sources[0].shape[1]
+def spread_slots(values, packed):
+    rows, width = values.shape
     slots = width // ARRAY_STATIONS
     lane = lax.broadcasted_iota(jnp.int32, (rows, LANES), 1)
     low = lane < ARRAY_STATIONS
@@ -29,40 +24,66 @@
     pair = 2 * ARRAY_STATIONS
     tail = jnp.zeros((rows, LANES - pair), jnp.float32)
     half = jnp.zeros((rows, LANES - ARRAY_STATIONS), jnp.float32)
-    for source_at, source in enumerate(sources):
-        values = source[...]
-        for at in range(slots // 2):
-            near = jnp.concatenate([values[:, at * pair : (at + 1) * pair], tail], axis=1)
-            far = pltpu.roll(near, PAD_STATIONS - ARRAY_STATIONS, axis=1)
-            packed[source_at, :, at * LANES : (at + 1) * LANES] = jnp.where(
-                low, near, jnp.where(high, far, 0.0)
-            )
-        packed[source_at, :, slots // 2 * LANES :] = jnp.concatenate(
-            [values[:, width - ARRAY_STATIONS :], half], axis=1
+    for at in range(slots // 2):
+        near = jnp.concatenate([values[:, at * pair : (at + 1) * pair], tail], axis=1)
+        far = pltpu.roll(near, PAD_STATIONS - ARRAY_STATIONS, axis=1)
+        packed[:, at * LANES : (at + 1) * LANES] = jnp.where(
+            low, near, jnp.where(high, far, 0.0)
         )
-    own = GAIN_SLOT_COUNT * PAD_STATIONS
-    window = own + PAD_STATIONS
+    packed[:, slots // 2 * LANES :] = jnp.concatenate(
+        [values[:, width - ARRAY_STATIONS :], half], axis=1
+    )
+
+
+def own_kernel(source, packed):
+    spread_slots(source[...], packed)
+
+
+def pack_kernel(*refs, npol, nbt, chans):
+    own = refs[0]
+    sources = refs[1:npol]
+    outs = refs[npol : npol + nbt]
+    scratch = refs[npol + nbt :]
+    bt = lax.axis_index("bt")
+    pol = lax.axis_index("pol")
+    for source, packed in zip(sources, scratch):
+        spread_slots(source[...], packed)
+    step = GAIN_SLOT_COUNT * PAD_STATIONS
+    window = step + PAD_STATIONS
     for shift in range(nbt):
         block = lax.rem(bt + shift, nbt) * npol + pol
-        start = pl.multiple_of(block * own, LANES)
-        for source_at in range(npol):
-            wide = packed[source_at, :, pl.ds(start, own + LANES)]
+        start = pl.multiple_of(block * step, LANES)
+        for source_at, packed in enumerate((own, *scratch)):
+            wide = packed[:, pl.ds(start, step + LANES)]
             outs[shift][source_at] = jnp.concatenate(
                 [wide[c * COMPS : (c + 1) * COMPS, :window] for c in range(chans)], axis=1
             )
+
+
+def prep_kernel(vis, first, second, tables, wide_vis):
+    per_slot = first.shape[1]
+    station = lax.broadcasted_iota(jnp.int32, (PAD_STATIONS, per_slot), 0)
+    position = lax.broadcasted_iota(jnp.int32, (PAD_STATIONS, per_slot), 1)
+    fraction = (position.astype(jnp.float32) + 0.5) / per_slot
+    rest = 1.0 - fraction
+    for slot in range(GAIN_SLOT_COUNT):
+        wide_vis[slot] = vis[:, slot * LANES : (slot + 1) * LANES].astype(jnp.float32)
+        for side, rows in enumerate((first, second)):
+            hit = station == rows[slot : slot + 1, :]
+            tables[slot, :, side * per_slot : (side + 1) * per_slot] = jnp.concatenate(
+                [jnp.where(hit, rest, 0.0), jnp.where(hit, fraction, 0.0)], axis=0
+            ).astype(jnp.bfloat16)
 
 
 def apply_kernel(*refs, npol, nbt, chans, facets, block_rows):
     facet_dir, filled = refs[:2]
     windows = refs[2 : 2 + nbt]
-    vis, first, second, out, facet_at, gathered, wide_vis, wide_out = refs[2 + nbt :]
+    tables, wide_vis, out, facet_at, gathered, wide_out = refs[2 + nbt :]
     bt = lax.axis_index("bt")
     pol = lax.axis_index("pol")
     per_slot = block_rows // GAIN_SLOT_COUNT
     for f in range(facets):
         facet_at[facet_dir[f]] = f
-    for slot in range(GAIN_SLOT_COUNT):
-        wide_vis[slot] = vis[:, slot * LANES : (slot + 1) * LANES].astype(jnp.float32)
     chunks = gathered.shape[0]
     for shift in range(nbt):
         for source_at in range(npol):
@@ -71,9 +92,9 @@
             )
             row = pl.multiple_of(facet_at[direction] * COMPS, COMPS)
             for chunk in range(chunks):
-                gathered[chunk, pl.ds(row, COMPS), :] = windows[shift][
-                    source_at, :, chunk * LANES : (chunk + 1) * LANES
-                ]
+                lanes = slice(chunk * LANES, (chunk + 1) * LANES)
+                piece = windows[shift][source_at, :, lanes]
+                gathered[chunk, pl.ds(row, COMPS), :] = piece
     gains = jnp.concatenate(
         [
             jnp.concatenate(
@@ -86,23 +107,11 @@
     coarse = gains.astype(jnp.bfloat16)
     fine = (gains - coarse.astype(jnp.float32)).astype(jnp.bfloat16)
     window = (GAIN_SLOT_COUNT + 1) * PAD_STATIONS
-    station = lax.broadcasted_iota(jnp.int32, (PAD_STATIONS, per_slot), 0)
-    position = lax.broadcasted_iota(jnp.int32, (PAD_STATIONS, per_slot), 1)
-    fraction = (position.astype(jnp.float32) + 0.5) / per_slot
-    rest = 1.0 - fraction
     place = lax.broadcasted_iota(jnp.int32, (facets, per_slot), 1)
     live_rows = filled[0]
 
-    def table_of(row):
-        hit = station == row
-        return jnp.concatenate(
-            [jnp.where(hit, rest, 0.0), jnp.where(hit, fraction, 0.0)], axis=0
-        ).astype(jnp.bfloat16)
-
     for slot in range(GAIN_SLOT_COUNT):
-        table = jnp.concatenate(
-            [table_of(first[slot : slot + 1, :]), table_of(second[slot : slot + 1, :])], axis=1
-        )
+        table = tables[slot]
         table = jnp.concatenate([table, table], axis=0)
         parts = []
         for c in range(chans):
@@ -162,6 +171,10 @@
     return pl.BlockSpec(memory_space=pltpu.VMEM)
 
 
+def in_vmem(array):
+    return pltpu.with_memory_space_constraint(array, pltpu.VMEM)
+
+
 def smem():
     return pl.BlockSpec(memory_space=pltpu.SMEM)
 
@@ -177,25 +190,43 @@
     slots = width // ARRAY_STATIONS
     window = chans * (GAIN_SLOT_COUNT + 1) * PAD_STATIONS
     flat = gains.reshape(chans * comps, width)
-    sources = [flat] + [
-        lax.ppermute(flat, "pol", [(i, (i + s) % npol) for i in range(npol)])
-        for s in range(1, npol)
-    ]
+    others = []
+    for k in range(1, npol):
+        others.append(lax.ppermute(flat, "pol", [(i, (i + k) % npol) for i in range(npol)]))
+    packed = (chans * comps, slots * PAD_STATIONS + LANES)
+    own = pl.pallas_call(
+        own_kernel,
+        out_shape=pltpu.VMEM(packed, jnp.float32),
+        in_specs=[vmem()],
+        out_specs=vmem(),
+        name="own_windows",
+    )(flat)
     outgoing = pl.pallas_call(
         functools.partial(pack_kernel, npol=npol, nbt=nbt, chans=chans),
-        out_shape=[jax.ShapeDtypeStruct((npol, comps, window), jnp.float32)] * nbt,
+        out_shape=[pltpu.VMEM((npol, comps, window), jnp.float32)] * nbt,
         in_specs=[vmem()] * npol,
         out_specs=[vmem()] * nbt,
-        scratch_shapes=[
-            pltpu.VMEM((npol, chans * comps, slots * PAD_STATIONS + LANES), jnp.float32)
+        scratch_shapes=[pltpu.VMEM(packed, jnp.float32)] * (npol - 1),
+        name="pack_windows",
+    )(in_vmem(own), *[in_vmem(s) for s in others])
+    arrived = [outgoing[0]]
+    for k in range(1, nbt):
+        arrived.append(lax.ppermute(outgoing[k], "bt", [(i, (i + k) % nbt) for i in range(nbt)]))
+    rows = facets * chans * comps
+    tables, wide_vis = pl.pallas_call(
+        prep_kernel,
+        out_shape=[
+            pltpu.VMEM((GAIN_SLOT_COUNT, 2 * PAD_STATIONS, 2 * per_slot), jnp.bfloat16),
+            pltpu.VMEM((GAIN_SLOT_COUNT, rows, LANES), jnp.float32),
         ],
-        name="pack_windows",
-    )(*sources)
-    arrived = [outgoing[0]] + [
-        lax.ppermute(outgoing[k], "bt", [(i, (i + k) % nbt) for i in range(nbt)])
-        for k in range(1, nbt)
-    ]
-    rows = facets * chans * comps
+        in_specs=[vmem()] * 3,
+        out_specs=[vmem()] * 2,
+        name="prepare",
+    )(
+        visibilities.reshape(rows, block_rows),
+        first_station.reshape(GAIN_SLOT_COUNT, per_slot),
+        second_station.reshape(GAIN_SLOT_COUNT, per_slot),
+    )
     corrected = pl.pallas_call(
         functools.partial(
             apply_kernel,
@@ -206,22 +237,20 @@
             block_rows=block_rows,
         ),
         out_shape=jax.ShapeDtypeStruct((rows, block_rows), jnp.bfloat16),
-        in_specs=[smem(), smem()] + [vmem()] * (nbt + 3),
+        in_specs=[smem(), smem()] + [vmem()] * (nbt + 2),
         out_specs=vmem(),
         scratch_shapes=[
             pltpu.SMEM((facets,), jnp.int32),
             pltpu.VMEM((window // LANES, facets * comps, LANES), jnp.float32),
-            pltpu.VMEM((GAIN_SLOT_COUNT, rows, LANES), jnp.float32),
             pltpu.VMEM((GAIN_SLOT_COUNT, rows, LANES), jnp.float32),
         ],
         name="apply_correction",
     )(
         facet_dir,
         filled_row_count,
-        *arrived,
-        visibilities.reshape(rows, block_rows),
-        first_station.reshape(GAIN_SLOT_COUNT, per_slot),
-        second_station.reshape(GAIN_SLOT_COUNT, per_slot),
+        *[in_vmem(a) for a in arrived],
+        in_vmem(tables),
+        in_vmem(wide_vis),
     )
     return corrected.reshape(visibilities.shape)
 

time: 17.4 us -> 13.5 us (0.78)
  waiting for transfers between devices: 3.39 us -> 1.1 us
  local copies, waits for them, and re-layouts: 1.27 us -> 0 us
  Pallas kernels: 4.59 us -> 4.14 us
    pallas_call x1, Pallas kernels: 2.44 us -> 0.29 us  [shards(): pl.pallas_call(functools.partial(pack_kernel, npol=npol, nbt=nbt, chans=c...]
    pallas_call x0 -> x2, Pallas kernels: none -> 2.08 us  [the longest x1 1.1 us: shards(): pl.pallas_call(own_kernel, out_shape=pltpu.VMEM(packed, jnp.float32), in_...]
    unnamed x8 -> x0, local copies, waits for them, and re-layouts: 1.27 us -> none
    ppermute x3, waiting for transfers between devices: 2.19 us -> 1.01 us  [shards(): lax.ppermute(outgoing[k], 'bt', [(i, (i + k) % nbt) for i in range(nbt)])]
    ppermute x1, waiting for transfers between devices: 1.2 us -> 0.09 us  [shards(): lax.ppermute(flat, 'pol', [(i, (i + k) % npol) for i in range(npol)])]
    pallas_call x1, Pallas kernels: 2.15 us -> 1.77 us  [shards(): pl.pallas_call(functools.partial(apply_kernel, npol=npol, nbt=nbt, chans=...]
  transfers between devices with their start and end apart: 4 -> 4, of which waited for: 3 -> 3; matrix products, arithmetic and copies ran while one was open for 0% -> 0% of each run, Pallas kernels for 0% -> 16%
where the time goes in v3:
time: 13.5 us; the launch traced here: 13.3 us
  starting transfers between devices  7.4 us (55%)
  Pallas kernels  4.14 us (31%)
  waiting for transfers between devices  1.1 us (8%)
  between operations  0.68 us (5%)
    ppermute x3, starting transfers between devices, shards(): lax.ppermute(outgoing[k], 'bt', [(i, (i + k) % nbt) for i in range(nbt)])  6.91 us
    pallas_call x1, Pallas kernels, shards(): pl.pallas_call(functools.partial(apply_kernel, npol=npol, nbt=nbt, chans=...  1.77 us
    pallas_call x1, Pallas kernels, shards(): pl.pallas_call(own_kernel, out_shape=pltpu.VMEM(packed, jnp.float32), in_...  1.1 us
    ppermute x3, waiting for transfers between devices, shards(): lax.ppermute(outgoing[k], 'bt', [(i, (i + k) % nbt) for i in range(nbt)])  1.01 us
    pallas_call x1, Pallas kernels, shards(): pl.pallas_call(prep_kernel, out_shape=[pltpu.VMEM((GAIN_SLOT_COUNT, 2 * P...  0.98 us
    ppermute x1, starting transfers between devices, shards(): lax.ppermute(flat, 'pol', [(i, (i + k) % npol) for i in range(npol)])  0.49 us
    pallas_call x1, Pallas kernels, shards(): pl.pallas_call(functools.partial(pack_kernel, npol=npol, nbt=nbt, chans=c...  0.29 us
  transfers between devices with their start and end apart: 4, of which 3 were waited for; matrix products, arithmetic and copies ran while one was open for 0% of the time, Pallas kernels for 16%

profile of v3, /device:TPU:0, one launch (start us, length us, event | category | flops | bytes accessed | tf_op | source)
XLA Modules:
  0.0 13.3 jit_solution(4137562670341476639)
XLA Ops:
  0.0 0.5 %collective-permute-start = (f32[16,1984]{1,0:T(8,128)}, f32[16,1984]{1,0:T(8,128)S(1)}, u32[]{:S(2)}, u32[]{:S(2)}) collective-permute-start(f32[16,1984]{1,0:T(8,128)} %bitcast.5), channel_id=1, source_target_pairs={{0,1},{1,0},{2,3},{3,2},{4,5},{5,4},{6,7},{7,6},{8,9},{9,8},{10,11... | collective-permute-start | bytes 380936 | tf_op jit(solution)/shard_map/ppermute | solution.py:195
  0.5 1.1 %own_windows.1.refs_0_ = f32[16,2176]{1,0:T(8,128)S(1)} custom-call(f32[16,1984]{1,0:T(8,128)} %bitcast.6), custom_call_target="tpu_custom_call" | custom-call | tf_op jit(solution)/shard_map/own_windows/pallas_call | solution.py:197
  1.6 0.1 collective-permute-done.refs_1_
  1.7 0.3 %pack_windows.1 = (f32[2,8,640]{2,1,0:T(8,128)S(1)}, f32[2,8,640]{2,1,0:T(8,128)S(1)}, f32[2,8,640]{2,1,0:T(8,128)S(1)}, f32[2,8,640]{2,1,0:T(8,128)S(1)}) custom-call(f32[16,2176]{1,0:T(8,128)S(1)} %own_windows.1.refs_0_, f32[16,1984]{1,0:T(8,128)S(1)} %collective-permute-done.refs_1_), custom_call_target="tpu_custom_call" | custom-call | tf_op jit(solution)/shard_map/pack_windows/pallas_call | solution.py:204
  2.0 3.0 %collective-permute-start.1 = (f32[2,8,640]{2,1,0:T(8,128)S(1)}, f32[2,8,640]{2,1,0:T(8,128)S(1)}, u32[]{:S(2)}, u32[]{:S(2)}) collective-permute-start(f32[2,8,640]{2,1,0:T(8,128)S(1)} %get-tuple-element.12), channel_id=1, source_target_pairs={{0,4},{4,8},{8,12},{12,0},{1,5},{5,9},{9,13},{13,1},{2,6},{6,10},{... | collective-permute-start | bytes 122888 | tf_op jit(solution)/shard_map/ppermute | solution.py:214
  5.0 2.6 %collective-permute-start.2 = (f32[2,8,640]{2,1,0:T(8,128)S(1)}, f32[2,8,640]{2,1,0:T(8,128)S(1)}, u32[]{:S(2)}, u32[]{:S(2)}) collective-permute-start(f32[2,8,640]{2,1,0:T(8,128)S(1)} %get-tuple-element.13), channel_id=1, source_target_pairs={{0,8},{4,12},{8,0},{12,4},{1,9},{5,13},{9,1},{13,5},{2,10},{6,14},... | collective-permute-start | bytes 122888 | tf_op jit(solution)/shard_map/ppermute | solution.py:214
  7.5 1.3 %collective-permute-start.3 = (f32[2,8,640]{2,1,0:T(8,128)S(1)}, f32[2,8,640]{2,1,0:T(8,128)S(1)}, u32[]{:S(2)}, u32[]{:S(2)}) collective-permute-start(f32[2,8,640]{2,1,0:T(8,128)S(1)} %get-tuple-element.14), channel_id=1, source_target_pairs={{0,12},{4,0},{8,4},{12,8},{1,13},{5,1},{9,5},{13,9},{2,14},{6,2},{... | collective-permute-start | bytes 122888 | tf_op jit(solution)/shard_map/ppermute | solution.py:214
  9.6 1.0 %prepare.1 = (bf16[4,128,256]{2,1,0:T(8,128)(2,1)S(1)}, f32[4,128,128]{2,1,0:T(8,128)S(1)}) custom-call(bf16[128,512]{1,0:T(8,128)(2,1)} %bitcast.7, s32[4,128]{1,0:T(4,128)} %bitcast.8, s32[4,128]{1,0:T(4,128)} %bitcast.9), custom_call_target="tpu_custom_call" | custom-call | tf_op jit(solution)/shard_map/prepare/pallas_call | solution.py:216
  10.5 0.0 collective-permute-done.1.refs_3_
  10.5 0.5 %collective-permute-done.2.refs_4_ = f32[2,8,640]{2,1,0:T(8,128)S(1)} collective-permute-done((f32[2,8,640]{2,1,0:T(8,128)S(1)}, f32[2,8,640]{2,1,0:T(8,128)S(1)}, u32[]{:S(2)}, u32[]{:S(2)}) %collective-permute-start.2) | collective-permute-done | bytes 40992 | tf_op jit(solution)/shard_map/ppermute | solution.py:214
  11.1 0.5 %collective-permute-done.3.refs_5_ = f32[2,8,640]{2,1,0:T(8,128)S(1)} collective-permute-done((f32[2,8,640]{2,1,0:T(8,128)S(1)}, f32[2,8,640]{2,1,0:T(8,128)S(1)}, u32[]{:S(2)}, u32[]{:S(2)}) %collective-permute-start.3) | collective-permute-done | bytes 40992 | tf_op jit(solution)/shard_map/ppermute | solution.py:214
  11.6 1.8 %apply_correction.1 = bf16[128,512]{1,0:T(8,128)(2,1)} custom-call(s32[8]{0:T(128)} %refs_0_.1, s32[1]{0:T(128)S(6)} %copy.7.refs_1_, f32[2,8,640]{2,1,0:T(8,128)S(1)} %get-tuple-element.11.refs_2_, f32[2,8,640]{2,1,0:T(8,128)S(1)} %collective-permute-done.1.refs_3_, f32[2,8,640]{2,1,0:T(8,128)S(1)} %collective-permute-done.2.refs_4_, ...), custom_call_target="tpu_custom_call" | custom-call | tf_op jit(solution)/shard_map/apply_correction/pallas_call | solution.py:230
Async XLA Ops:
  0.0 1.7 %collective-permute-start = (f32[16,1984]{1,0:T(8,128)}, f32[16,1984]{1,0:T(8,128)S(1)}, u32[]{:S(2)}, u32[]{:S(2)}) collective-permute-start(f32[16,1984]{1,0:T(8,128)} %bitcast.5), channel_id=1, source_target_pairs={{0,1},{1,0},{2,3},{3,2},{4,5},{5,4},{6,7},{7,6},{8,9},{9,8},{10,11... | collective-permute-start | bytes 380936 | tf_op jit(solution)/shard_map/ppermute | solution.py:195
  2.0 8.6 %collective-permute-start.1 = (f32[2,8,640]{2,1,0:T(8,128)S(1)}, f32[2,8,640]{2,1,0:T(8,128)S(1)}, u32[]{:S(2)}, u32[]{:S(2)}) collective-permute-start(f32[2,8,640]{2,1,0:T(8,128)S(1)} %get-tuple-element.12), channel_id=1, source_target_pairs={{0,4},{4,8},{8,12},{12,0},{1,5},{5,9},{9,13},{13,1},{2,6},{6,10},{... | collective-permute-start | bytes 122888 | tf_op jit(solution)/shard_map/ppermute | solution.py:214
  5.0 6.1 %collective-permute-start.2 = (f32[2,8,640]{2,1,0:T(8,128)S(1)}, f32[2,8,640]{2,1,0:T(8,128)S(1)}, u32[]{:S(2)}, u32[]{:S(2)}) collective-permute-start(f32[2,8,640]{2,1,0:T(8,128)S(1)} %get-tuple-element.13), channel_id=1, source_target_pairs={{0,8},{4,12},{8,0},{12,4},{1,9},{5,13},{9,1},{13,5},{2,10},{6,14},... | collective-permute-start | bytes 122888 | tf_op jit(solution)/shard_map/ppermute | solution.py:214
  7.5 4.0 %collective-permute-start.3 = (f32[2,8,640]{2,1,0:T(8,128)S(1)}, f32[2,8,640]{2,1,0:T(8,128)S(1)}, u32[]{:S(2)}, u32[]{:S(2)}) collective-permute-start(f32[2,8,640]{2,1,0:T(8,128)S(1)} %get-tuple-element.14), channel_id=1, source_target_pairs={{0,12},{4,0},{8,4},{12,8},{1,13},{5,1},{9,5},{13,9},{2,14},{6,2},{... | collective-permute-start | bytes 122888 | tf_op jit(solution)/shard_map/ppermute | solution.py:214

commit v4 on v3

--- a/solution.py
+++ b/solution.py
@@ -60,7 +60,11 @@
             )
 
 
-def prep_kernel(vis, first, second, tables, wide_vis):
+def prep_kernel(facet_dir, filled, vis, first, second, plan, tables, wide_vis):
+    facets = facet_dir.shape[0]
+    for f in range(facets):
+        plan[facet_dir[f]] = f
+    plan[facets] = filled[0]
     per_slot = first.shape[1]
     station = lax.broadcasted_iota(jnp.int32, (PAD_STATIONS, per_slot), 0)
     position = lax.broadcasted_iota(jnp.int32, (PAD_STATIONS, per_slot), 1)
@@ -76,21 +80,19 @@
 
 
 def apply_kernel(*refs, npol, nbt, chans, facets, block_rows):
-    facet_dir, filled = refs[:2]
-    windows = refs[2 : 2 + nbt]
-    tables, wide_vis, out, facet_at, gathered, wide_out = refs[2 + nbt :]
+    plan = refs[0]
+    windows = refs[1 : 1 + nbt]
+    tables, wide_vis, out, gathered, wide_out = refs[1 + nbt :]
     bt = lax.axis_index("bt")
     pol = lax.axis_index("pol")
     per_slot = block_rows // GAIN_SLOT_COUNT
-    for f in range(facets):
-        facet_at[facet_dir[f]] = f
     chunks = gathered.shape[0]
     for shift in range(nbt):
         for source_at in range(npol):
             direction = lax.rem(bt - shift + nbt, nbt) * npol + lax.rem(
                 pol - source_at + npol, npol
             )
-            row = pl.multiple_of(facet_at[direction] * COMPS, COMPS)
+            row = pl.multiple_of(plan[direction] * COMPS, COMPS)
             for chunk in range(chunks):
                 lanes = slice(chunk * LANES, (chunk + 1) * LANES)
                 piece = windows[shift][source_at, :, lanes]
@@ -108,7 +110,7 @@
     fine = (gains - coarse.astype(jnp.float32)).astype(jnp.bfloat16)
     window = (GAIN_SLOT_COUNT + 1) * PAD_STATIONS
     place = lax.broadcasted_iota(jnp.int32, (facets, per_slot), 1)
-    live_rows = filled[0]
+    live_rows = plan[facets]
 
     for slot in range(GAIN_SLOT_COUNT):
         table = tables[slot]
@@ -213,16 +215,19 @@
     for k in range(1, nbt):
         arrived.append(lax.ppermute(outgoing[k], "bt", [(i, (i + k) % nbt) for i in range(nbt)]))
     rows = facets * chans * comps
-    tables, wide_vis = pl.pallas_call(
+    plan, tables, wide_vis = pl.pallas_call(
         prep_kernel,
         out_shape=[
+            pltpu.SMEM((facets + 1,), jnp.int32),
             pltpu.VMEM((GAIN_SLOT_COUNT, 2 * PAD_STATIONS, 2 * per_slot), jnp.bfloat16),
             pltpu.VMEM((GAIN_SLOT_COUNT, rows, LANES), jnp.float32),
         ],
-        in_specs=[vmem()] * 3,
-        out_specs=[vmem()] * 2,
+        in_specs=[smem()] * 2 + [vmem()] * 3,
+        out_specs=[smem()] + [vmem()] * 2,
         name="prepare",
     )(
+        facet_dir,
+        filled_row_count,
         visibilities.reshape(rows, block_rows),
         first_station.reshape(GAIN_SLOT_COUNT, per_slot),
         second_station.reshape(GAIN_SLOT_COUNT, per_slot),
@@ -237,17 +242,15 @@
             block_rows=block_rows,
         ),
         out_shape=jax.ShapeDtypeStruct((rows, block_rows), jnp.bfloat16),
-        in_specs=[smem(), smem()] + [vmem()] * (nbt + 2),
+        in_specs=[smem()] + [vmem()] * (nbt + 2),
         out_specs=vmem(),
         scratch_shapes=[
-            pltpu.SMEM((facets,), jnp.int32),
             pltpu.VMEM((window // LANES, facets * comps, LANES), jnp.float32),
             pltpu.VMEM((GAIN_SLOT_COUNT, rows, LANES), jnp.float32),
         ],
         name="apply_correction",
     )(
-        facet_dir,
-        filled_row_count,
+        pltpu.with_memory_space_constraint(plan, pltpu.SMEM),
         *[in_vmem(a) for a in arrived],
         in_vmem(tables),
         in_vmem(wide_vis),

time: 13.5 us -> 12.8 us (0.948)
  Pallas kernels: 4.14 us -> 3.48 us
    pallas_call x1, Pallas kernels: 1.77 us -> 1.11 us  [shards(): pl.pallas_call(functools.partial(apply_kernel, npol=npol, nbt=nbt, chans=...]
where the time goes in v4:
time: 12.8 us; the launch traced here: 12.7 us
  starting transfers between devices  7.4 us (58%)
  Pallas kernels  3.48 us (27%)
  waiting for transfers between devices  1.08 us (8%)
  between operations  0.69 us (5%)
    ppermute x3, starting transfers between devices, shards(): lax.ppermute(outgoing[k], 'bt', [(i, (i + k) % nbt) for i in range(nbt)])  6.91 us
    pallas_call x1, Pallas kernels, shards(): pl.pallas_call(functools.partial(apply_kernel, npol=npol, nbt=nbt, chans=...  1.11 us
    pallas_call x1, Pallas kernels, shards(): pl.pallas_call(own_kernel, out_shape=pltpu.VMEM(packed, jnp.float32), in_...  1.1 us
    ppermute x3, waiting for transfers between devices, shards(): lax.ppermute(outgoing[k], 'bt', [(i, (i + k) % nbt) for i in range(nbt)])  1 us
    pallas_call x1, Pallas kernels, shards(): pl.pallas_call(prep_kernel, out_shape=[pltpu.SMEM((facets + 1,), jnp.int3...  0.99 us
    ppermute x1, starting transfers between devices, shards(): lax.ppermute(flat, 'pol', [(i, (i + k) % npol) for i in range(npol)])  0.49 us
    pallas_call x1, Pallas kernels, shards(): pl.pallas_call(functools.partial(pack_kernel, npol=npol, nbt=nbt, chans=c...  0.29 us
  transfers between devices with their start and end apart: 4, of which 3 were waited for; matrix products, arithmetic and copies ran while one was open for 0% of the time, Pallas kernels for 16%

profile of v4, /device:TPU:0, one launch (start us, length us, event | category | flops | bytes accessed | tf_op | source)
XLA Modules:
  0.0 12.7 jit_solution(13966089426647898964)
XLA Ops:
  0.0 0.5 %collective-permute-start = (f32[16,1984]{1,0:T(8,128)}, f32[16,1984]{1,0:T(8,128)S(1)}, u32[]{:S(2)}, u32[]{:S(2)}) collective-permute-start(f32[16,1984]{1,0:T(8,128)} %bitcast.5), channel_id=1, source_target_pairs={{0,1},{1,0},{2,3},{3,2},{4,5},{5,4},{6,7},{7,6},{8,9},{9,8},{10,11... | collective-permute-start | bytes 380936 | tf_op jit(solution)/shard_map/ppermute | solution.py:197
  0.5 1.1 %own_windows.1.refs_0_ = f32[16,2176]{1,0:T(8,128)S(1)} custom-call(f32[16,1984]{1,0:T(8,128)} %bitcast.6), custom_call_target="tpu_custom_call" | custom-call | tf_op jit(solution)/shard_map/own_windows/pallas_call | solution.py:199
  1.6 0.1 collective-permute-done.refs_1_
  1.7 0.3 %pack_windows.1 = (f32[2,8,640]{2,1,0:T(8,128)S(1)}, f32[2,8,640]{2,1,0:T(8,128)S(1)}, f32[2,8,640]{2,1,0:T(8,128)S(1)}, f32[2,8,640]{2,1,0:T(8,128)S(1)}) custom-call(f32[16,2176]{1,0:T(8,128)S(1)} %own_windows.1.refs_0_, f32[16,1984]{1,0:T(8,128)S(1)} %collective-permute-done.refs_1_), custom_call_target="tpu_custom_call" | custom-call | tf_op jit(solution)/shard_map/pack_windows/pallas_call | solution.py:206
  2.0 3.0 %collective-permute-start.1 = (f32[2,8,640]{2,1,0:T(8,128)S(1)}, f32[2,8,640]{2,1,0:T(8,128)S(1)}, u32[]{:S(2)}, u32[]{:S(2)}) collective-permute-start(f32[2,8,640]{2,1,0:T(8,128)S(1)} %get-tuple-element.14), channel_id=1, source_target_pairs={{0,4},{4,8},{8,12},{12,0},{1,5},{5,9},{9,13},{13,1},{2,6},{6,10},{... | collective-permute-start | bytes 122888 | tf_op jit(solution)/shard_map/ppermute | solution.py:216
  5.0 2.6 %collective-permute-start.2 = (f32[2,8,640]{2,1,0:T(8,128)S(1)}, f32[2,8,640]{2,1,0:T(8,128)S(1)}, u32[]{:S(2)}, u32[]{:S(2)}) collective-permute-start(f32[2,8,640]{2,1,0:T(8,128)S(1)} %get-tuple-element.15), channel_id=1, source_target_pairs={{0,8},{4,12},{8,0},{12,4},{1,9},{5,13},{9,1},{13,5},{2,10},{6,14},... | collective-permute-start | bytes 122888 | tf_op jit(solution)/shard_map/ppermute | solution.py:216
  7.5 1.3 %collective-permute-start.3 = (f32[2,8,640]{2,1,0:T(8,128)S(1)}, f32[2,8,640]{2,1,0:T(8,128)S(1)}, u32[]{:S(2)}, u32[]{:S(2)}) collective-permute-start(f32[2,8,640]{2,1,0:T(8,128)S(1)} %get-tuple-element.16), channel_id=1, source_target_pairs={{0,12},{4,0},{8,4},{12,8},{1,13},{5,1},{9,5},{13,9},{2,14},{6,2},{... | collective-permute-start | bytes 122888 | tf_op jit(solution)/shard_map/ppermute | solution.py:216
  9.5 1.0 %prepare.1 = (s32[9]{0:T(128)S(4)}, bf16[4,128,256]{2,1,0:T(8,128)(2,1)S(1)}, f32[4,128,128]{2,1,0:T(8,128)S(1)}) custom-call(s32[8]{0:T(128)} %facet_dir.1, s32[1]{0:T(128)S(6)} %copy.7.filled, bf16[128,512]{1,0:T(8,128)(2,1)} %bitcast.7, s32[4,128]{1,0:T(4,128)} %bitcast.8, s32[4,128]{1,0:T(4,128)} %bitcast.9), custom_call_target="tpu_custom_call" | custom-call | tf_op jit(solution)/shard_map/prepare/pallas_call | solution.py:218
  10.5 0.0 collective-permute-done.1.refs_2_
  10.6 0.5 %collective-permute-done.2.refs_3_ = f32[2,8,640]{2,1,0:T(8,128)S(1)} collective-permute-done((f32[2,8,640]{2,1,0:T(8,128)S(1)}, f32[2,8,640]{2,1,0:T(8,128)S(1)}, u32[]{:S(2)}, u32[]{:S(2)}) %collective-permute-start.2) | collective-permute-done | bytes 40992 | tf_op jit(solution)/shard_map/ppermute | solution.py:216
  11.1 0.5 %collective-permute-done.3.refs_4_ = f32[2,8,640]{2,1,0:T(8,128)S(1)} collective-permute-done((f32[2,8,640]{2,1,0:T(8,128)S(1)}, f32[2,8,640]{2,1,0:T(8,128)S(1)}, u32[]{:S(2)}, u32[]{:S(2)}) %collective-permute-start.3) | collective-permute-done | bytes 40992 | tf_op jit(solution)/shard_map/ppermute | solution.py:216
  11.6 1.1 %apply_correction.1 = bf16[128,512]{1,0:T(8,128)(2,1)} custom-call(s32[9]{0:T(128)S(4)} %get-tuple-element.12.refs_0_, f32[2,8,640]{2,1,0:T(8,128)S(1)} %get-tuple-element.13.refs_1_, f32[2,8,640]{2,1,0:T(8,128)S(1)} %collective-permute-done.1.refs_2_, f32[2,8,640]{2,1,0:T(8,128)S(1)} %collective-permute-done.2.refs_3_, ...), custom_call_target="tpu_custom_call" | custom-call | tf_op jit(solution)/shard_map/apply_correction/pallas_call | solution.py:235
Async XLA Ops:
  0.0 1.7 %collective-permute-start = (f32[16,1984]{1,0:T(8,128)}, f32[16,1984]{1,0:T(8,128)S(1)}, u32[]{:S(2)}, u32[]{:S(2)}) collective-permute-start(f32[16,1984]{1,0:T(8,128)} %bitcast.5), channel_id=1, source_target_pairs={{0,1},{1,0},{2,3},{3,2},{4,5},{5,4},{6,7},{7,6},{8,9},{9,8},{10,11... | collective-permute-start | bytes 380936 | tf_op jit(solution)/shard_map/ppermute | solution.py:197
  2.0 8.6 %collective-permute-start.1 = (f32[2,8,640]{2,1,0:T(8,128)S(1)}, f32[2,8,640]{2,1,0:T(8,128)S(1)}, u32[]{:S(2)}, u32[]{:S(2)}) collective-permute-start(f32[2,8,640]{2,1,0:T(8,128)S(1)} %get-tuple-element.14), channel_id=1, source_target_pairs={{0,4},{4,8},{8,12},{12,0},{1,5},{5,9},{9,13},{13,1},{2,6},{6,10},{... | collective-permute-start | bytes 122888 | tf_op jit(solution)/shard_map/ppermute | solution.py:216
  5.0 6.1 %collective-permute-start.2 = (f32[2,8,640]{2,1,0:T(8,128)S(1)}, f32[2,8,640]{2,1,0:T(8,128)S(1)}, u32[]{:S(2)}, u32[]{:S(2)}) collective-permute-start(f32[2,8,640]{2,1,0:T(8,128)S(1)} %get-tuple-element.15), channel_id=1, source_target_pairs={{0,8},{4,12},{8,0},{12,4},{1,9},{5,13},{9,1},{13,5},{2,10},{6,14},... | collective-permute-start | bytes 122888 | tf_op jit(solution)/shard_map/ppermute | solution.py:216
  7.5 4.0 %collective-permute-start.3 = (f32[2,8,640]{2,1,0:T(8,128)S(1)}, f32[2,8,640]{2,1,0:T(8,128)S(1)}, u32[]{:S(2)}, u32[]{:S(2)}) collective-permute-start(f32[2,8,640]{2,1,0:T(8,128)S(1)} %get-tuple-element.16), channel_id=1, source_target_pairs={{0,12},{4,0},{8,4},{12,8},{1,13},{5,1},{9,5},{13,9},{2,14},{6,2},{... | collective-permute-start | bytes 122888 | tf_op jit(solution)/shard_map/ppermute | solution.py:216

commit v5 on v4

--- a/solution.py
+++ b/solution.py
@@ -35,29 +35,36 @@
     )
 
 
-def own_kernel(source, packed):
+def window_of(packed, block, chans):
+    step = GAIN_SLOT_COUNT * PAD_STATIONS
+    wide = packed[:, pl.ds(pl.multiple_of(block * step, LANES), step + LANES)]
+    return jnp.concatenate(
+        [wide[c * COMPS : (c + 1) * COMPS, : step + PAD_STATIONS] for c in range(chans)], axis=1
+    )
+
+
+def own_kernel(source, packed, lead, *, npol, nbt, chans):
+    bt = lax.axis_index("bt")
+    pol = lax.axis_index("pol")
     spread_slots(source[...], packed)
+    for s in range(npol):
+        block = lax.rem(bt + 1, nbt) * npol + lax.rem(pol + s, npol)
+        lead[s] = window_of(packed, block, chans)
 
 
 def pack_kernel(*refs, npol, nbt, chans):
     own = refs[0]
     sources = refs[1:npol]
-    outs = refs[npol : npol + nbt]
-    scratch = refs[npol + nbt :]
+    outs = refs[npol : npol + nbt - 1]
+    scratch = refs[npol + nbt - 1 :]
     bt = lax.axis_index("bt")
     pol = lax.axis_index("pol")
     for source, packed in zip(sources, scratch):
         spread_slots(source[...], packed)
-    step = GAIN_SLOT_COUNT * PAD_STATIONS
-    window = step + PAD_STATIONS
-    for shift in range(nbt):
+    for out, shift in zip(outs, [0, *range(2, nbt)]):
         block = lax.rem(bt + shift, nbt) * npol + pol
-        start = pl.multiple_of(block * step, LANES)
         for source_at, packed in enumerate((own, *scratch)):
-            wide = packed[:, pl.ds(start, step + LANES)]
-            outs[shift][source_at] = jnp.concatenate(
-                [wide[c * COMPS : (c + 1) * COMPS, :window] for c in range(chans)], axis=1
-            )
+            out[source_at] = window_of(packed, block, chans)
 
 
 def prep_kernel(facet_dir, filled, vis, first, second, plan, tables, wide_vis):
@@ -82,7 +89,8 @@
 def apply_kernel(*refs, npol, nbt, chans, facets, block_rows):
     plan = refs[0]
     windows = refs[1 : 1 + nbt]
-    tables, wide_vis, out, gathered, wide_out = refs[1 + nbt :]
+    late = refs[1 + nbt : nbt + npol]
+    tables, wide_vis, out, gathered, wide_out = refs[nbt + npol :]
     bt = lax.axis_index("bt")
     pol = lax.axis_index("pol")
     per_slot = block_rows // GAIN_SLOT_COUNT
@@ -95,7 +103,10 @@
             row = pl.multiple_of(plan[direction] * COMPS, COMPS)
             for chunk in range(chunks):
                 lanes = slice(chunk * LANES, (chunk + 1) * LANES)
-                piece = windows[shift][source_at, :, lanes]
+                if shift == 1 and source_at:
+                    piece = late[source_at - 1][:, lanes]
+                else:
+                    piece = windows[shift][source_at, :, lanes]
                 gathered[chunk, pl.ds(row, COMPS), :] = piece
     gains = jnp.concatenate(
         [
@@ -196,24 +207,28 @@
     for k in range(1, npol):
         others.append(lax.ppermute(flat, "pol", [(i, (i + k) % npol) for i in range(npol)]))
     packed = (chans * comps, slots * PAD_STATIONS + LANES)
-    own = pl.pallas_call(
-        own_kernel,
-        out_shape=pltpu.VMEM(packed, jnp.float32),
+    own, lead = pl.pallas_call(
+        functools.partial(own_kernel, npol=npol, nbt=nbt, chans=chans),
+        out_shape=[pltpu.VMEM(packed, jnp.float32), pltpu.VMEM((npol, comps, window), jnp.float32)],
         in_specs=[vmem()],
-        out_specs=vmem(),
+        out_specs=[vmem()] * 2,
         name="own_windows",
     )(flat)
     outgoing = pl.pallas_call(
         functools.partial(pack_kernel, npol=npol, nbt=nbt, chans=chans),
-        out_shape=[pltpu.VMEM((npol, comps, window), jnp.float32)] * nbt,
+        out_shape=[pltpu.VMEM((npol, comps, window), jnp.float32)] * (nbt - 1),
         in_specs=[vmem()] * npol,
-        out_specs=[vmem()] * nbt,
+        out_specs=[vmem()] * (nbt - 1),
         scratch_shapes=[pltpu.VMEM(packed, jnp.float32)] * (npol - 1),
         name="pack_windows",
     )(in_vmem(own), *[in_vmem(s) for s in others])
+    outgoing = [outgoing[0], lead, *outgoing[1:]]
     arrived = [outgoing[0]]
     for k in range(1, nbt):
         arrived.append(lax.ppermute(outgoing[k], "bt", [(i, (i + k) % nbt) for i in range(nbt)]))
+    late = []
+    for k in range(1, npol):
+        late.append(lax.ppermute(arrived[1][k], "pol", [(i, (i + k) % npol) for i in range(npol)]))
     rows = facets * chans * comps
     plan, tables, wide_vis = pl.pallas_call(
         prep_kernel,
@@ -242,7 +257,7 @@
             block_rows=block_rows,
         ),
         out_shape=jax.ShapeDtypeStruct((rows, block_rows), jnp.bfloat16),
-        in_specs=[smem()] + [vmem()] * (nbt + 2),
+        in_specs=[smem()] + [vmem()] * (nbt + npol + 1),
         out_specs=vmem(),
         scratch_shapes=[
             pltpu.VMEM((window // LANES, facets * comps, LANES), jnp.float32),
@@ -251,7 +266,7 @@
         name="apply_correction",
     )(
         pltpu.with_memory_space_constraint(plan, pltpu.SMEM),
-        *[in_vmem(a) for a in arrived],
+        *[in_vmem(a) for a in arrived + late],
         in_vmem(tables),
         in_vmem(wide_vis),
     )

time: 12.8 us -> 12.4 us (0.969)
  starting transfers between devices: 7.4 us -> 7.06 us
    ppermute x3, starting transfers between devices: 6.91 us -> 6.57 us  [shards(): lax.ppermute(outgoing[k], 'bt', [(i, (i + k) % nbt) for i in range(nbt)])]
  transfers between devices with their start and end apart: 4 -> 5, of which waited for: 3 -> 1; matrix products, arithmetic and copies ran while one was open for 0% -> 0% of each run, Pallas kernels for 16% -> 20%
where the time goes in v5:
time: 12.4 us; the launch traced here: 12.3 us
  starting transfers between devices  7.06 us (57%)
  Pallas kernels  3.56 us (29%)
  waiting for transfers between devices  0.98 us (8%)
  between operations  0.69 us (6%)
    ppermute x3, starting transfers between devices, shards(): lax.ppermute(outgoing[k], 'bt', [(i, (i + k) % nbt) for i in range(nbt)])  6.57 us
    pallas_call x1, Pallas kernels, shards(): pl.pallas_call(functools.partial(own_kernel, npol=npol, nbt=nbt, chans=ch...  1.18 us
    pallas_call x1, Pallas kernels, shards(): pl.pallas_call(functools.partial(apply_kernel, npol=npol, nbt=nbt, chans=...  1.11 us
    pallas_call x1, Pallas kernels, shards(): pl.pallas_call(prep_kernel, out_shape=[pltpu.SMEM((facets + 1,), jnp.int3...  0.99 us
    ppermute x3, waiting for transfers between devices, shards(): lax.ppermute(outgoing[k], 'bt', [(i, (i + k) % nbt) for i in range(nbt)])  0.98 us
    ppermute x1, starting transfers between devices, shards(): lax.ppermute(flat, 'pol', [(i, (i + k) % npol) for i in range(npol)])  0.49 us
    pallas_call x1, Pallas kernels, shards(): pl.pallas_call(functools.partial(pack_kernel, npol=npol, nbt=nbt, chans=c...  0.28 us
  transfers between devices with their start and end apart: 5, of which 1 were waited for; matrix products, arithmetic and copies ran while one was open for 0% of the time, Pallas kernels for 20%

profile of v5, /device:TPU:0, one launch (start us, length us, event | category | flops | bytes accessed | tf_op | source)
XLA Modules:
  0.0 12.3 jit_solution(9385116825863352387)
XLA Ops:
  0.0 0.5 %collective-permute-start = (f32[16,1984]{1,0:T(8,128)}, f32[16,1984]{1,0:T(8,128)S(1)}, u32[]{:S(2)}, u32[]{:S(2)}) collective-permute-start(f32[16,1984]{1,0:T(8,128)} %bitcast.7), channel_id=1, source_target_pairs={{0,1},{1,0},{2,3},{3,2},{4,5},{5,4},{6,7},{7,6},{8,9},{9,8},{10,11... | collective-permute-start | bytes 380936 | tf_op jit(solution)/shard_map/ppermute | solution.py:208
  0.5 1.2 %own_windows.1 = (f32[16,2176]{1,0:T(8,128)S(1)}, f32[2,8,640]{2,1,0:T(8,128)S(1)}) custom-call(f32[16,1984]{1,0:T(8,128)} %bitcast.8), custom_call_target="tpu_custom_call" | custom-call | tf_op jit(solution)/shard_map/own_windows/pallas_call | solution.py:210
  1.7 2.6 %collective-permute-start.1 = (f32[2,8,640]{2,1,0:T(8,128)S(1)}, f32[2,8,640]{2,1,0:T(8,128)S(1)}, u32[]{:S(2)}, u32[]{:S(2)}) collective-permute-start(f32[2,8,640]{2,1,0:T(8,128)S(1)} %get-tuple-element.16), channel_id=1, source_target_pairs={{0,4},{4,8},{8,12},{12,0},{1,5},{5,9},{9,13},{13,1},{2,6},{6,10},{... | collective-permute-start | bytes 122888 | tf_op jit(solution)/shard_map/ppermute | solution.py:228
  4.2 0.0 collective-permute-done.refs_1_
  4.2 0.3 %pack_windows.1 = (f32[2,8,640]{2,1,0:T(8,128)S(1)}, f32[2,8,640]{2,1,0:T(8,128)S(1)}, f32[2,8,640]{2,1,0:T(8,128)S(1)}) custom-call(f32[16,2176]{1,0:T(8,128)S(1)} %get-tuple-element.14.refs_0_, f32[16,1984]{1,0:T(8,128)S(1)} %collective-permute-done.refs_1_), custom_call_target="tpu_custom_call" | custom-call | tf_op jit(solution)/shard_map/pack_windows/pallas_call | solution.py:217
  4.5 2.7 %collective-permute-start.2 = (f32[2,8,640]{2,1,0:T(8,128)S(1)}, f32[2,8,640]{2,1,0:T(8,128)S(1)}, u32[]{:S(2)}, u32[]{:S(2)}) collective-permute-start(f32[2,8,640]{2,1,0:T(8,128)S(1)} %get-tuple-element.17), channel_id=1, source_target_pairs={{0,8},{4,12},{8,0},{12,4},{1,9},{5,13},{9,1},{13,5},{2,10},{6,14},... | collective-permute-start | bytes 122888 | tf_op jit(solution)/shard_map/ppermute | solution.py:228
  7.2 1.4 %collective-permute-start.3 = (f32[2,8,640]{2,1,0:T(8,128)S(1)}, f32[2,8,640]{2,1,0:T(8,128)S(1)}, u32[]{:S(2)}, u32[]{:S(2)}) collective-permute-start(f32[2,8,640]{2,1,0:T(8,128)S(1)} %get-tuple-element.18), channel_id=1, source_target_pairs={{0,12},{4,0},{8,4},{12,8},{1,13},{5,1},{9,5},{13,9},{2,14},{6,2},{... | collective-permute-start | bytes 122888 | tf_op jit(solution)/shard_map/ppermute | solution.py:228
  8.5 0.0 collective-permute-done.1.refs_2_
  8.5 0.0 collective-permute-start.4
  9.2 1.0 %prepare.1 = (s32[9]{0:T(128)S(4)}, bf16[4,128,256]{2,1,0:T(8,128)(2,1)S(1)}, f32[4,128,128]{2,1,0:T(8,128)S(1)}) custom-call(s32[8]{0:T(128)} %facet_dir.1, s32[1]{0:T(128)S(6)} %copy.7.filled, bf16[128,512]{1,0:T(8,128)(2,1)} %bitcast.9, s32[4,128]{1,0:T(4,128)} %bitcast.10, s32[4,128]{1,0:T(4,128)} %bitcast.11), custom_call_target="tpu_custom_call" | custom-call | tf_op jit(solution)/shard_map/prepare/pallas_call | solution.py:233
  10.2 0.0 collective-permute-done.4.refs_5_
  10.2 0.0 collective-permute-done.2.refs_3_
  10.2 1.0 %collective-permute-done.3.refs_4_ = f32[2,8,640]{2,1,0:T(8,128)S(1)} collective-permute-done((f32[2,8,640]{2,1,0:T(8,128)S(1)}, f32[2,8,640]{2,1,0:T(8,128)S(1)}, u32[]{:S(2)}, u32[]{:S(2)}) %collective-permute-start.3) | collective-permute-done | bytes 40992 | tf_op jit(solution)/shard_map/ppermute | solution.py:228
  11.2 1.1 %apply_correction.1 = bf16[128,512]{1,0:T(8,128)(2,1)} custom-call(s32[9]{0:T(128)S(4)} %get-tuple-element.13.refs_0_, f32[2,8,640]{2,1,0:T(8,128)S(1)} %get-tuple-element.15.refs_1_, f32[2,8,640]{2,1,0:T(8,128)S(1)} %collective-permute-done.1.refs_2_, f32[2,8,640]{2,1,0:T(8,128)S(1)} %collective-permute-done.2.refs_3_, ...), custom_call_target="tpu_custom_call" | custom-call | tf_op jit(solution)/shard_map/apply_correction/pallas_call | solution.py:250
  (1 shorter events, 0.0 us)
Async XLA Ops:
  0.0 4.2 %collective-permute-start = (f32[16,1984]{1,0:T(8,128)}, f32[16,1984]{1,0:T(8,128)S(1)}, u32[]{:S(2)}, u32[]{:S(2)}) collective-permute-start(f32[16,1984]{1,0:T(8,128)} %bitcast.7), channel_id=1, source_target_pairs={{0,1},{1,0},{2,3},{3,2},{4,5},{5,4},{6,7},{7,6},{8,9},{9,8},{10,11... | collective-permute-start | bytes 380936 | tf_op jit(solution)/shard_map/ppermute | solution.py:208
  1.7 6.9 %collective-permute-start.1 = (f32[2,8,640]{2,1,0:T(8,128)S(1)}, f32[2,8,640]{2,1,0:T(8,128)S(1)}, u32[]{:S(2)}, u32[]{:S(2)}) collective-permute-start(f32[2,8,640]{2,1,0:T(8,128)S(1)} %get-tuple-element.16), channel_id=1, source_target_pairs={{0,4},{4,8},{8,12},{12,0},{1,5},{5,9},{9,13},{13,1},{2,6},{6,10},{... | collective-permute-start | bytes 122888 | tf_op jit(solution)/shard_map/ppermute | solution.py:228
  4.5 5.7 %collective-permute-start.2 = (f32[2,8,640]{2,1,0:T(8,128)S(1)}, f32[2,8,640]{2,1,0:T(8,128)S(1)}, u32[]{:S(2)}, u32[]{:S(2)}) collective-permute-start(f32[2,8,640]{2,1,0:T(8,128)S(1)} %get-tuple-element.17), channel_id=1, source_target_pairs={{0,8},{4,12},{8,0},{12,4},{1,9},{5,13},{9,1},{13,5},{2,10},{6,14},... | collective-permute-start | bytes 122888 | tf_op jit(solution)/shard_map/ppermute | solution.py:228
  7.2 4.0 %collective-permute-start.3 = (f32[2,8,640]{2,1,0:T(8,128)S(1)}, f32[2,8,640]{2,1,0:T(8,128)S(1)}, u32[]{:S(2)}, u32[]{:S(2)}) collective-permute-start(f32[2,8,640]{2,1,0:T(8,128)S(1)} %get-tuple-element.18), channel_id=1, source_target_pairs={{0,12},{4,0},{8,4},{12,8},{1,13},{5,1},{9,5},{13,9},{2,14},{6,2},{... | collective-permute-start | bytes 122888 | tf_op jit(solution)/shard_map/ppermute | solution.py:228
  8.5 1.7 %collective-permute-start.4 = (f32[8,640]{1,0:T(8,128)S(1)}, f32[8,640]{1,0:T(8,128)S(1)}, u32[]{:S(2)}, u32[]{:S(2)}) collective-permute-start(f32[8,640]{1,0:T(8,128)S(1)} %slice_bitcast_fusion), channel_id=1, source_target_pairs={{0,1},{1,0},{2,3},{3,2},{4,5},{5,4},{6,7},{7,6},{8,9},{9,8},{10,11... | collective-permute-start | bytes 61448 | tf_op jit(solution)/shard_map/ppermute | solution.py:231
